TPU v7x, 512 devices: a whole 4x8x8 slice. The times are simulated.
512 devices in a mesh: sec: 32 (over x, y), day: 16 (over z, core).
Axes of the slice: x: 4, y: 8, z: 8, core: 2. Of those that a mesh axis runs over, the one named last changes fastest.
Arguments:
- sec_pnl: bfloat16 [32768, 2048], P('sec', 'day'), may hold values from -6 to 6
- holdings: bfloat16 [512, 128, 128], P('sec'), may hold values from -0.0546875 to 0.0546875
- tile_pblock: int32 [512], P('sec'), may hold values from 0 to 1, as said below
- tile_sblock: int32 [512], P('sec'), may hold values from 0 to 7
- tile_count: int32 [32], P('sec'), may hold values from 4 to 16, as said below
- tail_days: int32 [256, 103], replicated, may hold values from 0 to 2047, as said below
Outputs:
- pnl: bfloat16 [256, 2048], P('sec', 'day')
- shortfall: float32 [256], P('sec')
- tail_mean: float32 [512, 128, 128], P(('sec', 'day'))
Inputs may be any that keep to these rules, and one draw needn't show every extreme that they name: On each security device the pairs (tile_pblock, tile_sblock) of its 16 slots are distinct. `tile_count`: some security device has all 16 slots live in every draw. `tail_days`: each row holds 103 distinct days.
All inputs are finite; a program needn't handle non-finite values.
Results may differ from a plain program's by a relative error of at most 0.0015.
Values may be sent and summed in bfloat16 or wider, within the bound.
No kernel may reach another device: no remote copies, remote signals or barrier semaphores. Data moves between devices by JAX's collectives and lax.ppermute only.
A program may use at most 64 MiB of HBM per device.

v0:
```python
import jax
import jax.numpy as jnp
from jax import lax
from jax.sharding import PartitionSpec as P

SB = 128
PB = 128
TAIL = 103


def in_blocks(shard, dim, peers):
    before, after = (shard.shape[:dim], shard.shape[dim + 1 :])
    return jnp.moveaxis(shard.reshape(*before, peers, -1, *after), dim, 0)


def sent_and_summed(shard, axis, dim):
    tiles = in_blocks(shard, dim, lax.axis_size(axis))
    arrived = lax.all_to_all(tiles, axis, split_axis=0, concat_axis=0, tiled=True)
    return arrived.sum(axis=0)


def from_everyone(shard, axis):
    copies = jnp.broadcast_to(shard, (lax.axis_size(axis), *shard.shape))
    return lax.all_to_all(copies, axis, split_axis=0, concat_axis=0, tiled=True)


def of_everyone(shard, axis):
    return from_everyone(shard, axis).sum(axis=0)


def mask_from_days(day_lists, first_day, width):
    span = 128
    count = width // span
    offsets = lax.broadcasted_iota(jnp.int32, (1, 1, span), 2)

    def one_span(which):
        start = first_day + which * span
        hits = day_lists[:, :, None] - start == offsets
        return jnp.any(hits, axis=1).astype(jnp.bfloat16)

    pieces = lax.map(one_span, jnp.arange(count, dtype=jnp.int32))
    return jnp.transpose(pieces, (1, 0, 2)).reshape(day_lists.shape[0], width)


def local(sec_pnl, holdings, tile_pblock, tile_sblock, tile_count, tail_days):
    n_day = lax.axis_size("day")
    days_dev = sec_pnl.shape[1]
    slots = holdings.shape[0]
    portfolios = tail_days.shape[0]
    pblocks = portfolios // PB
    blocks = sec_pnl.reshape(-1, SB, days_dev)
    count = tile_count[0]
    alive = (jnp.arange(slots, dtype=jnp.int32) < count).astype(jnp.float32)
    first_day = lax.axis_index("day") * days_dev
    tail_mask = mask_from_days(tail_days, first_day, days_dev)
    selected = jnp.take(blocks, tile_sblock, axis=0)
    products = jnp.einsum("tps,tsd->tpd", holdings, selected, preferred_element_type=jnp.float32)
    owner = (tile_pblock[None, :] == jnp.arange(pblocks, dtype=jnp.int32)[:, None]).astype(
        jnp.float32
    ) * alive[None, :]
    partial_value = jnp.dot(
        owner,
        products.reshape(slots, -1),
        precision=lax.Precision.HIGHEST,
        preferred_element_type=jnp.float32,
    ).reshape(portfolios, days_dev)
    share = sent_and_summed(partial_value, "sec", 0)
    pnl = share.astype(jnp.bfloat16)
    row_start = lax.axis_index("sec") * share.shape[0]
    my_mask = lax.dynamic_slice_in_dim(tail_mask, row_start, share.shape[0], 0).astype(jnp.float32)
    picked = jnp.sum(my_mask * share, axis=1)
    shortfall = -of_everyone(picked, "day") / TAIL
    per_device = slots // n_day
    own_start = lax.axis_index("day") * per_device
    mask_blocks = tail_mask.reshape(pblocks, PB, days_dev)
    left = jnp.take(mask_blocks, tile_pblock, axis=0)
    right = jnp.take(blocks, tile_sblock, axis=0)
    summed = sent_and_summed(
        jnp.einsum("tpd,tsd->tps", left, right, preferred_element_type=jnp.float32), "day", 0
    )
    own_alive = lax.dynamic_slice_in_dim(alive, own_start, per_device)
    tail_mean = summed * own_alive[:, None, None] / TAIL
    return (pnl, shortfall, tail_mean)


def solution(mesh):
    placed = (P("sec", "day"), P("sec", None, None), P("sec"), P("sec"), P("sec"), P())
    return jax.shard_map(
        local,
        mesh=mesh,
        in_specs=placed,
        out_specs=(P("sec", "day"), P("sec"), P(("sec", "day"), None, None)),
        check_vma=False,
    )
```

profile of v0, /device:TPU:1, one launch (start us, length us, event | category | flops | bytes accessed | tf_op | source)
XLA Modules:
  0.0 81.2 jit_solution(16171209032392052583)
XLA Ops:
  0.6 0.0 copy-start
  0.6 0.7 compare_select_fusion
  1.4 0.7 compare_and_fusion
  2.0 1.6 %gather_fusion.1 = bf16[16,128,128]{2,1,0:T(8,128)(2,1)S(1)} fusion(bf16[8,128,128]{2,1,0:T(8,128)(2,1)} %bitcast.20, s32[1024]{0:T(1024)S(1)} %pad_clamp_fusion.1), kind=kCustom, calls=%fused_computation.clone | custom fusion | bytes 1048640 | tf_op jit(solution)/shard_map/jit(_take)/gather | solution.py:56
  3.6 0.7 convolution_bitcast_fusion.1
  4.3 0.3 copy.22
  4.7 0.0 copy-start.1
  5.4 1.2 %fusion.1 = f32[2,16384]{1,0:T(2,128)S(1)} fusion(f32[2,8,128,128]{3,2,1,0:T(8,128)S(1)} %bitcast.19, f32[16]{0:T(128)S(1)} %compare_convert_fusion, s32[16]{0:T(128)S(1)} %copy-done.2), kind=kOutput, calls=%fused_computation.6 | convolution fusion | flops 6291520 | bytes 1179776 | tf_op jit(solution)/shard_map/dot_general | solution.py:61
  6.6 0.8 reshape_reshape.3
  7.3 10.5 %all-to-all-start = ((f32[32,8,128]{2,1,0:T(8,128)}), f32[32,8,128]{2,1,0:T(8,128)S(1)}, u32[]{:S(2)}, u32[]{:S(2)}) async-start(f32[32,8,128]{2,1,0:T(8,128)} %reshape_reshape.3), calls=%async_computation | async-start | bytes 262144 | tf_op jit(solution)/shard_map/all_to_all | solution.py:18
  17.9 4.8 %fusion = pred[256,128]{1,0:T(8,128)(4,1)S(1)} fusion(s32[256,103]{0,1:T(8,128)S(1)} %broadcast_subtract_fusion), kind=kLoop, calls=%fused_computation.3 | loop fusion | flops 6717440 | bytes 138240 | tf_op jit(solution)/shard_map/while/body/eval_jaxpr/reduce_or | solution.py:39
  22.7 0.6 gather_fusion
  23.4 3.6 %all-to-all-done = f32[32,8,128]{2,1,0:T(8,128)S(1)} async-done(((f32[32,8,128]{2,1,0:T(8,128)}), f32[32,8,128]{2,1,0:T(8,128)S(1)}, u32[]{:S(2)}, u32[]{:S(2)}) %all-to-all-start) | async-done | bytes 131104 | tf_op jit(solution)/shard_map/all_to_all | solution.py:18
  27.0 0.7 multiply_reduce_fusion
  27.7 0.6 broadcast_in_dim.34
  28.3 12.4 %all-to-all-start.1 = ((f32[16,1,8]{2,1,0:T(1,128)}), f32[16,1,8]{2,1,0:T(1,128)S(1)}, u32[]{:S(2)}, u32[]{:S(2)}) async-start(f32[16,1,8]{2,1,0:T(1,128)} %broadcast_in_dim.34), calls=%async_computation.1 | async-start | bytes 16384 | tf_op jit(solution)/shard_map/all_to_all | solution.py:24
  40.7 1.6 %convolution_bitcast_fusion = f32[16,1,128,128]{3,2,1,0:T(8,128)} fusion(bf16[16,128,128]{2,1,0:T(8,128)(2,1)S(1)} %gather_fusion, pred[16]{0:T(512)(128)(4,1)S(1)} %compare_and_fusion.1, bf16[16,128,128]{2,1,0:T(8,128)(2,1)S(1)} %gather_fusion.1, pred[16]{0:T(512)(128)(4,1)S(1)} %compare_and_fusion), kind=kOutput, calls=%fused_computation.4 | convolution fusion | flops 67633152 | bytes 2097184 | tf_op jit(solution)/shard_map/tpd,tsd->tps/dot_general | solution.py:79
  42.3 5.4 %all-to-all-done.1 = f32[16,1,8]{2,1,0:T(1,128)S(1)} async-done(((f32[16,1,8]{2,1,0:T(1,128)}), f32[16,1,8]{2,1,0:T(1,128)S(1)}, u32[]{:S(2)}, u32[]{:S(2)}) %all-to-all-start.1) | async-done | bytes 544 | tf_op jit(solution)/shard_map/all_to_all | solution.py:24
  47.7 4.1 %all-to-all-start.2 = ((f32[16,1,128,128]{3,2,1,0:T(8,128)}), f32[16,1,128,128]{3,2,1,0:T(8,128)S(1)}, u32[]{:S(2)}, u32[]{:S(2)}) async-start(f32[16,1,128,128]{3,2,1,0:T(8,128)} %convolution_bitcast_fusion), calls=%async_computation.2 | async-start | bytes 2097152 | tf_op jit(solution)/shard_map/all_to_all | solution.py:18
  51.8 0.7 dynamic_slice.10
  52.5 0.5 negate_multiply_fusion
  53.0 26.8 %all-to-all-done.2 = f32[16,1,128,128]{3,2,1,0:T(8,128)S(1)} async-done(((f32[16,1,128,128]{3,2,1,0:T(8,128)}), f32[16,1,128,128]{3,2,1,0:T(8,128)S(1)}, u32[]{:S(2)}, u32[]{:S(2)}) %all-to-all-start.2) | async-done | bytes 1048608 | tf_op jit(solution)/shard_map/all_to_all | solution.py:18
  79.8 0.1 reduce_sum.39
  79.9 1.3 %multiply_bitcast_fusion = f32[1,128,128]{2,1,0:T(8,128)} fusion(f32[128,128]{1,0:T(8,128)S(1)} %reduce_sum.39, f32[]{:T(128)} %bitcast.6), kind=kLoop, calls=%fused_computation.13 | loop fusion | flops 32768 | bytes 131076 | tf_op jit(solution)/shard_map/div | solution.py:82
  (13 shorter events, 0.1 us)
Async XLA Ops:
  0.6 3.0 %copy-start = (bf16[16,128,128]{2,1,0:T(8,128)(2,1)S(1)}, bf16[16,128,128]{2,1,0:T(8,128)(2,1)}, u32[]{:S(2)}) copy-start(bf16[16,128,128]{2,1,0:T(8,128)(2,1)} %param.9) | copy-start | bytes 1572868
  4.3 1.1 %copy-start.2 = (s32[16]{0:T(128)S(1)}, s32[16]{0:T(128)}, u32[]{:S(2)}) copy-start(s32[16]{0:T(128)} %param.10) | copy-start | bytes 196
  4.7 13.2 %copy-start.1 = (s32[256,103]{0,1:T(8,128)S(1)}, s32[256,103]{0,1:T(8,128)}, u32[]{:S(2)}) copy-start(s32[256,103]{0,1:T(8,128)} %param.13) | copy-start | bytes 316420
  7.3 19.7 %all-to-all-start = ((f32[32,8,128]{2,1,0:T(8,128)}), f32[32,8,128]{2,1,0:T(8,128)S(1)}, u32[]{:S(2)}, u32[]{:S(2)}) async-start(f32[32,8,128]{2,1,0:T(8,128)} %reshape_reshape.3), calls=%async_computation | async-start | bytes 262144 | tf_op jit(solution)/shard_map/all_to_all | solution.py:18
  28.3 19.4 %all-to-all-start.1 = ((f32[16,1,8]{2,1,0:T(1,128)}), f32[16,1,8]{2,1,0:T(1,128)S(1)}, u32[]{:S(2)}, u32[]{:S(2)}) async-start(f32[16,1,8]{2,1,0:T(1,128)} %broadcast_in_dim.34), calls=%async_computation.1 | async-start | bytes 16384 | tf_op jit(solution)/shard_map/all_to_all | solution.py:24
  47.7 32.1 %all-to-all-start.2 = ((f32[16,1,128,128]{3,2,1,0:T(8,128)}), f32[16,1,128,128]{3,2,1,0:T(8,128)S(1)}, u32[]{:S(2)}, u32[]{:S(2)}) async-start(f32[16,1,128,128]{3,2,1,0:T(8,128)} %convolution_bitcast_fusion), calls=%async_computation.2 | async-start | bytes 2097152 | tf_op jit(solution)/shard_map/all_to_all | solution.py:18
where the time goes:
time: 81.6 us; the launch traced here: 81.2 us
  waiting for transfers between devices  35.9 us (44%)
  starting transfers between devices  27 us (33%)
  other arithmetic  8.87 us (11%)
  local copies, waits for them, and re-layouts  4.62 us (6%)
  matrix products  3.41 us (4%)
  between operations  1.47 us (2%)
    all_to_all x2, waiting for transfers between devices, sent_and_summed(): lax.all_to_all(tiles, axis, split_axis=0, concat_axis=0, tiled=True)  30.4 us
    all_to_all x2, starting transfers between devices, sent_and_summed(): lax.all_to_all(tiles, axis, split_axis=0, concat_axis=0, tiled=True)  14.6 us
    all_to_all x1, starting transfers between devices, from_everyone(): return lax.all_to_all(copies, axis, split_axis=0, concat_axis=0, tiled=True)  12.4 us
    all_to_all x1, waiting for transfers between devices, from_everyone(): return lax.all_to_all(copies, axis, split_axis=0, concat_axis=0, tiled=True)  5.42 us
    reduce_or x1, other arithmetic, one_span(): return jnp.any(hits, axis=1).astype(jnp.bfloat16)  4.77 us
  transfers between devices with their start and end apart: 3, of which 3 were waited for; matrix products, arithmetic and copies ran while one was open for 10% of the time, Pallas kernels for 0%

commit v1 on v0

v1 whole, which is shorter than its diff:
```python
import functools

import jax
import jax.numpy as jnp
from jax import lax
from jax.experimental import pallas as pl
from jax.experimental.pallas import tpu as pltpu
from jax.sharding import PartitionSpec as P

SB = 128
PB = 128
TAIL = 103
LIMIT = 4 * 1024 * 1024
VMEM = pltpu.VMEM
SMEM = pltpu.SMEM


def spec(space):
    return pl.BlockSpec(memory_space=space)


def exchange(x, axis):
    return lax.all_to_all(x, axis, split_axis=0, concat_axis=0, tiled=True)


def partial_kernel(pb, sb, cnt, sec, hold, out, inv):
    slots = hold.shape[0]
    nsb = sec.shape[0] // SB
    npb = slots // nsb
    for t in range(slots):
        inv[pb[t] * nsb + sb[t]] = t
    for p in range(npb):
        acc = None
        for s in range(nsb):
            t = inv[p * nsb + s]
            live = (t < cnt[0]).astype(jnp.float32)
            term = live * jnp.dot(hold[t], sec[s * SB : (s + 1) * SB, :], preferred_element_type=jnp.float32)
            acc = term if acc is None else acc + term
        out[p * PB : (p + 1) * PB, :] = acc


def gather_kernel(sb, sec, out):
    for t in range(out.shape[0]):
        out[t] = sec[pl.ds(pl.multiple_of(sb[t] * SB, SB), SB), :]


def mask_kernel(pb, days, words, mine, turned):
    width = mine.shape[1]
    k = lax.axis_index("day")
    q = lax.axis_index("sec")
    nw = words.shape[0]
    first = k * width
    row = q * mine.shape[0]
    own = pl.ds(pl.multiple_of(pb[k] * PB, PB), PB)
    near = pl.ds(pl.multiple_of((row // PB) * PB, PB), PB)
    iw = lax.broadcasted_iota(jnp.int32, (nw, PB), 0)
    i8 = lax.broadcasted_iota(jnp.int32, (8, PB), 0)
    one = jnp.int32(1)
    acc = jnp.zeros((nw, PB), jnp.int32)
    loc = jnp.zeros((8, PB), jnp.int32)
    for j in range(0, TAIL, 8):
        n = min(8, TAIL - j)
        far = days[j : j + n, own]
        w = far & (nw - 1)
        b = lax.shift_left(jnp.full((n, PB), one), far // nw)
        here = days[j : j + n, near] - first
        inside = (here >= 0) & (here < width)
        hw = jnp.where(inside, here & 7, 8)
        hb = lax.shift_left(jnp.full((n, PB), one), jnp.where(inside, here // 8, 0))
        for r in range(n):
            acc = acc | jnp.where(iw == w[r : r + 1], b[r : r + 1], 0)
            loc = loc | jnp.where(i8 == hw[r : r + 1], hb[r : r + 1], 0)
    words[...] = acc
    local = jnp.concatenate([((loc >> b) & 1).astype(jnp.float32) for b in range(width // 8)], axis=0)
    turned[...] = local.T
    mine[...] = turned[pl.ds(pl.multiple_of(row % PB, 8), mine.shape[0]), :]


def share_kernel(arrived, mine, pnl, sums):
    share = jnp.sum(arrived[...], axis=0)
    pnl[...] = share.astype(jnp.bfloat16)
    picked = jnp.sum(share * mine[...], axis=1, keepdims=True)
    shape = share.shape
    diag = lax.broadcasted_iota(jnp.int32, shape, 0) == lax.broadcasted_iota(jnp.int32, shape, 1)
    line = jnp.sum(jnp.where(diag, picked, 0.0), axis=0, keepdims=True)
    for k in range(sums.shape[0]):
        sums[k] = line


def tail_kernel(cnt, words, blocks, out):
    bits = words[...]
    nw = bits.shape[0]
    per = SB // nw
    acc = None
    for k in range(blocks.shape[0]):
        mask = jnp.concatenate([((bits >> (k * per + i)) & 1).astype(jnp.float32) for i in range(per)], axis=0)
        term = jnp.dot(blocks[k], mask.astype(jnp.bfloat16), preferred_element_type=jnp.float32)
        acc = term if acc is None else acc + term
    live = (lax.axis_index("day") < cnt[0]).astype(jnp.float32)
    out[0] = acc.T * live / TAIL


def local(sec_pnl, holdings, tile_pblock, tile_sblock, tile_count, tail_days):
    n_day = lax.axis_size("day")
    n_sec = lax.axis_size("sec")
    width = sec_pnl.shape[1]
    slots = holdings.shape[0]
    portfolios = tail_days.shape[0]
    rows = portfolios // n_sec
    f32 = jnp.float32
    partial = pl.pallas_call(
        partial_kernel,
        out_shape=jax.ShapeDtypeStruct((portfolios, width), f32),
        in_specs=[spec(SMEM)] * 3 + [spec(VMEM)] * 2,
        out_specs=spec(VMEM),
        scratch_shapes=[pltpu.SMEM((slots,), jnp.int32)],
        cost_estimate=pl.CostEstimate(flops=2 * slots * SB * PB * width, bytes_accessed=900000, transcendentals=0),
        compiler_params=pltpu.CompilerParams(vmem_limit_bytes=LIMIT),
        name="partial",
    )(tile_pblock, tile_sblock, tile_count, sec_pnl, holdings)
    arrived = exchange(partial.reshape(n_sec, rows, width), "sec")
    selected = pl.pallas_call(
        gather_kernel,
        out_shape=jax.ShapeDtypeStruct((slots, SB, width), jnp.bfloat16),
        in_specs=[spec(SMEM), spec(VMEM)],
        out_specs=spec(VMEM),
        cost_estimate=pl.CostEstimate(flops=10**7, bytes_accessed=800000, transcendentals=0),
        compiler_params=pltpu.CompilerParams(vmem_limit_bytes=LIMIT),
        name="gather",
    )(tile_sblock, sec_pnl)
    blocks = exchange(selected, "day")
    words, mine = pl.pallas_call(
        mask_kernel,
        out_shape=(jax.ShapeDtypeStruct((n_day * width // 32, PB), jnp.int32), jax.ShapeDtypeStruct((rows, width), f32)),
        in_specs=[spec(SMEM), spec(VMEM)],
        out_specs=(spec(VMEM), spec(VMEM)),
        scratch_shapes=[pltpu.VMEM((PB, width), f32)],
        cost_estimate=pl.CostEstimate(flops=10**7, bytes_accessed=200000, transcendentals=0),
        compiler_params=pltpu.CompilerParams(vmem_limit_bytes=LIMIT),
        name="mask",
    )(tile_pblock, tail_days.T)
    pnl, sums = pl.pallas_call(
        share_kernel,
        out_shape=(jax.ShapeDtypeStruct((rows, width), jnp.bfloat16), jax.ShapeDtypeStruct((n_day, 1, 128), f32)),
        in_specs=[spec(VMEM)] * 2,
        out_specs=(spec(VMEM), spec(VMEM)),
        cost_estimate=pl.CostEstimate(flops=10**5, bytes_accessed=200000, transcendentals=0),
        compiler_params=pltpu.CompilerParams(vmem_limit_bytes=LIMIT),
        name="share",
    )(arrived, mine)
    total = exchange(sums, "day")
    shortfall = -(jnp.sum(total, axis=(0, 1))[:rows]) / TAIL
    tail_mean = pl.pallas_call(
        tail_kernel,
        out_shape=jax.ShapeDtypeStruct((1, PB, SB), f32),
        in_specs=[spec(SMEM)] + [spec(VMEM)] * 2,
        out_specs=spec(VMEM),
        cost_estimate=pl.CostEstimate(flops=2 * slots * SB * PB * width, bytes_accessed=700000, transcendentals=0),
        compiler_params=pltpu.CompilerParams(vmem_limit_bytes=LIMIT),
        name="tail",
    )(tile_count, words, blocks)
    return pnl, shortfall, tail_mean


def solution(mesh):
    placed = (P("sec", "day"), P("sec", None, None), P("sec"), P("sec"), P("sec"), P())
    return jax.shard_map(
        local,
        mesh=mesh,
        in_specs=placed,
        out_specs=(P("sec", "day"), P("sec"), P(("sec", "day"), None, None)),
        check_vma=False,
    )
```

time: 81.6 us -> 67.5 us (0.83)
  other arithmetic: 8.87 us -> 0.55 us
  Pallas kernels: 0 us -> 5.75 us
  waiting for transfers between devices: 35.9 us -> 30.3 us
  matrix products: 3.41 us -> 0 us
  local copies, waits for them, and re-layouts: 4.62 us -> 2 us
    pallas_call x0 -> x5, Pallas kernels: none -> 5.75 us  [the longest x1 1.49 us: local(): pl.pallas_call(partial_kernel, out_shape=jax.ShapeDtypeStruct((portfolios...]
    all_to_all x3, waiting for transfers between devices: 35.9 us -> 30.3 us  [exchange(): return lax.all_to_all(x, axis, split_axis=0, concat_axis=0, tiled=True)]
    reduce_or x1 -> x0, other arithmetic: 4.77 us -> none  [one_span(): return jnp.any(hits, axis=1).astype(jnp.bfloat16)]
    dot_general x3 -> x0, matrix products: 3.41 us -> none  [the longest x1 1.55 us: local(): jnp.einsum('tpd,tsd->tps', left, right, preferred_element_type=jnp.float32)]
    gather x2 -> x0, local copies, waits for them, and re-layouts: 2.25 us -> none  [the longest x1 1.6 us: local(): selected = jnp.take(blocks, tile_sblock, axis=0)]
    unnamed x6 -> x12, local copies, waits for them, and re-layouts: 0.02 us -> 2 us
    div x2 -> x1, other arithmetic: 1.84 us -> 0.52 us  [local(): shortfall = -jnp.sum(total, axis=(0, 1))[:rows] / TAIL]
  transfers between devices with their start and end apart: 3 -> 3, of which waited for: 3 -> 3; matrix products, arithmetic and copies ran while one was open for 10% -> 1% of each run, Pallas kernels for 0% -> 4%
where the time goes in v1:
time: 67.5 us; the launch traced here: 67.1 us
  waiting for transfers between devices  30.3 us (45%)
  starting transfers between devices  27 us (40%)
  Pallas kernels  5.75 us (9%)
  local copies, waits for them, and re-layouts  2 us (3%)
  between operations  1.37 us (2%)
    all_to_all x3, waiting for transfers between devices, exchange(): return lax.all_to_all(x, axis, split_axis=0, concat_axis=0, tiled=True)  30.3 us
    all_to_all x3, starting transfers between devices, exchange(): return lax.all_to_all(x, axis, split_axis=0, concat_axis=0, tiled=True)  27 us
    unnamed x12, local copies, waits for them, and re-layouts  2 us
    pallas_call x1, Pallas kernels, local(): pl.pallas_call(partial_kernel, out_shape=jax.ShapeDtypeStruct((portfolios...  1.49 us
    pallas_call x1, Pallas kernels, local(): pl.pallas_call(gather_kernel, out_shape=jax.ShapeDtypeStruct((slots, SB,...  1.37 us
  transfers between devices with their start and end apart: 3, of which 3 were waited for; matrix products, arithmetic and copies ran while one was open for 1% of the time, Pallas kernels for 4%

profile of v1, /device:TPU:1, one launch (start us, length us, event | category | flops | bytes accessed | tf_op | source)
XLA Modules:
  0.0 67.1 jit_solution(11859856826860492884)
XLA Ops:
  0.6 0.0 copy-start.5
  0.6 0.0 copy-start.4
  1.3 0.0 copy-done.5
  1.3 0.0 copy-done.4
  1.3 0.0 copy-start
  1.3 0.9 %copy-done = bf16[1024,128]{1,0:T(8,128)(2,1)S(1)} copy-done((bf16[1024,128]{1,0:T(8,128)(2,1)S(1)}, bf16[1024,128]{1,0:T(8,128)(2,1)}, u32[]{:S(2)}) %copy-start) | copy-done | bytes 262168
  2.3 0.0 copy-start.2
  2.3 1.0 %copy-done.2 = bf16[16,128,128]{2,1,0:T(8,128)(2,1)S(1)} copy-done((bf16[16,128,128]{2,1,0:T(8,128)(2,1)S(1)}, bf16[16,128,128]{2,1,0:T(8,128)(2,1)}, u32[]{:S(2)}) %copy-start.2) | copy-done | bytes 524312
  3.3 0.0 copy-start.3
  3.3 1.5 %partial.1 = f32[256,128]{1,0:T(8,128)} custom-call(s32[16]{0:T(128)S(1)} %copy-done.4, s32[16]{0:T(128)S(1)} %copy-done.5, s32[1]{0:T(128)S(6)} %copy.9.cnt, bf16[1024,128]{1,0:T(8,128)(2,1)S(1)} %copy-done, bf16[16,128,128]{2,1,0:T(8,128)(2,1)S(1)} %copy-done.2), custom_call_target="tpu_custom_call" | custom-call | flops 67108864 | bytes 900000 | tf_op jit(solution)/shard_map/partial/pallas_call | solution.py:111
  4.8 0.0 copy-start.1
  4.8 10.6 %all-to-all-start = ((f32[32,8,128]{2,1,0:T(8,128)}), f32[32,8,128]{2,1,0:T(8,128)S(1)}, u32[]{:S(2)}, u32[]{:S(2)}) async-start(f32[32,8,128]{2,1,0:T(8,128)} %bitcast), calls=%async_computation | async-start | bytes 262144 | tf_op jit(solution)/shard_map/all_to_all | solution.py:23
  15.5 0.0 copy-done.3
  15.5 1.1 %mask.1 = (s32[64,128]{1,0:T(8,128)S(1)}, f32[8,128]{1,0:T(8,128)S(1)}) custom-call(s32[16]{0:T(128)S(1)} %copy-done.4, s32[103,256]{1,0:T(8,128)S(1)} %bitcast.2), custom_call_target="tpu_custom_call" | custom-call | flops 10000000 | bytes 200000 | tf_op jit(solution)/shard_map/mask/pallas_call | solution.py:132
  16.6 8.0 %all-to-all-done.arrived = f32[32,8,128]{2,1,0:T(8,128)S(1)} async-done(((f32[32,8,128]{2,1,0:T(8,128)}), f32[32,8,128]{2,1,0:T(8,128)S(1)}, u32[]{:S(2)}, u32[]{:S(2)}) %all-to-all-start) | async-done | bytes 131104 | tf_op jit(solution)/shard_map/all_to_all | solution.py:23
  24.6 0.7 %share.1 = (bf16[8,128]{1,0:T(8,128)(2,1)}, f32[16,1,128]{2,1,0:T(1,128)}) custom-call(f32[32,8,128]{2,1,0:T(8,128)S(1)} %all-to-all-done.arrived, f32[8,128]{1,0:T(8,128)S(1)} %get-tuple-element.7.mine), custom_call_target="tpu_custom_call" | custom-call | flops 100000 | bytes 200000 | tf_op jit(solution)/shard_map/share/pallas_call | solution.py:142
  25.3 12.4 %all-to-all-start.1 = ((f32[16,1,128]{2,1,0:T(1,128)}), f32[16,1,128]{2,1,0:T(1,128)S(1)}, u32[]{:S(2)}, u32[]{:S(2)}) async-start(f32[16,1,128]{2,1,0:T(1,128)} %get-tuple-element.9), calls=%async_computation.1 | async-start | bytes 16384 | tf_op jit(solution)/shard_map/all_to_all | solution.py:23
  37.7 0.0 copy-done.1
  37.7 1.4 %gather.1 = bf16[16,128,128]{2,1,0:T(8,128)(2,1)} custom-call(s32[16]{0:T(128)S(1)} %copy-done.5, bf16[1024,128]{1,0:T(8,128)(2,1)S(1)} %copy-done.1), custom_call_target="tpu_custom_call" | custom-call | flops 10000000 | bytes 800000 | tf_op jit(solution)/shard_map/gather/pallas_call | solution.py:122
  39.1 5.6 %all-to-all-done.1 = f32[16,1,128]{2,1,0:T(1,128)S(1)} async-done(((f32[16,1,128]{2,1,0:T(1,128)}), f32[16,1,128]{2,1,0:T(1,128)S(1)}, u32[]{:S(2)}, u32[]{:S(2)}) %all-to-all-start.1) | async-done | bytes 8224 | tf_op jit(solution)/shard_map/all_to_all | solution.py:23
  44.7 4.0 %all-to-all-start.2 = ((bf16[16,128,128]{2,1,0:T(8,128)(2,1)}), bf16[16,128,128]{2,1,0:T(8,128)(2,1)S(1)}, u32[]{:S(2)}, u32[]{:S(2)}) async-start(bf16[16,128,128]{2,1,0:T(8,128)(2,1)} %gather.1), calls=%async_computation.2 | async-start | bytes 1048576 | tf_op jit(solution)/shard_map/all_to_all | solution.py:23
  48.8 0.5 negate_multiply_fusion
  49.3 16.8 %all-to-all-done.2.blocks = bf16[16,128,128]{2,1,0:T(8,128)(2,1)S(1)} async-done(((bf16[16,128,128]{2,1,0:T(8,128)(2,1)}), bf16[16,128,128]{2,1,0:T(8,128)(2,1)S(1)}, u32[]{:S(2)}, u32[]{:S(2)}) %all-to-all-start.2) | async-done | bytes 524320 | tf_op jit(solution)/shard_map/all_to_all | solution.py:23
  66.0 1.0 %tail.1 = f32[1,128,128]{2,1,0:T(8,128)} custom-call(s32[1]{0:T(128)S(6)} %copy.9.cnt, s32[64,128]{1,0:T(8,128)S(1)} %get-tuple-element.10.words, bf16[16,128,128]{2,1,0:T(8,128)(2,1)S(1)} %all-to-all-done.2.blocks), custom_call_target="tpu_custom_call" | custom-call | flops 67108864 | bytes 700000 | tf_op jit(solution)/shard_map/tail/pallas_call | solution.py:153
  (1 shorter events, 0.0 us)
Async XLA Ops:
  0.6 0.7 %copy-start.5 = (s32[16]{0:T(128)S(1)}, s32[16]{0:T(128)}, u32[]{:S(2)}) copy-start(s32[16]{0:T(128)} %sb.3) | copy-start | bytes 196
  0.6 0.7 %copy-start.4 = (s32[16]{0:T(128)S(1)}, s32[16]{0:T(128)}, u32[]{:S(2)}) copy-start(s32[16]{0:T(128)} %pb.3) | copy-start | bytes 196
  1.3 1.0 %copy-start = (bf16[1024,128]{1,0:T(8,128)(2,1)S(1)}, bf16[1024,128]{1,0:T(8,128)(2,1)}, u32[]{:S(2)}) copy-start(bf16[1024,128]{1,0:T(8,128)(2,1)} %sec.3) | copy-start | bytes 786436
  2.3 1.0 %copy-start.2 = (bf16[16,128,128]{2,1,0:T(8,128)(2,1)S(1)}, bf16[16,128,128]{2,1,0:T(8,128)(2,1)}, u32[]{:S(2)}) copy-start(bf16[16,128,128]{2,1,0:T(8,128)(2,1)} %hold.1) | copy-start | bytes 1572868
  3.3 12.1 %copy-start.3 = (s32[256,103]{0,1:T(8,128)S(1)}, s32[256,103]{0,1:T(8,128)}, u32[]{:S(2)}) copy-start(s32[256,103]{0,1:T(8,128)} %param.11) | copy-start | bytes 316420
  4.8 32.9 %copy-start.1 = (bf16[1024,128]{1,0:T(8,128)(2,1)S(1)}, bf16[1024,128]{1,0:T(8,128)(2,1)}, u32[]{:S(2)}) copy-start(bf16[1024,128]{1,0:T(8,128)(2,1)} %sec.3) | copy-start | bytes 786436
  4.8 19.8 %all-to-all-start = ((f32[32,8,128]{2,1,0:T(8,128)}), f32[32,8,128]{2,1,0:T(8,128)S(1)}, u32[]{:S(2)}, u32[]{:S(2)}) async-start(f32[32,8,128]{2,1,0:T(8,128)} %bitcast), calls=%async_computation | async-start | bytes 262144 | tf_op jit(solution)/shard_map/all_to_all | solution.py:23
  25.3 19.4 %all-to-all-start.1 = ((f32[16,1,128]{2,1,0:T(1,128)}), f32[16,1,128]{2,1,0:T(1,128)S(1)}, u32[]{:S(2)}, u32[]{:S(2)}) async-start(f32[16,1,128]{2,1,0:T(1,128)} %get-tuple-element.9), calls=%async_computation.1 | async-start | bytes 16384 | tf_op jit(solution)/shard_map/all_to_all | solution.py:23
  44.7 21.3 %all-to-all-start.2 = ((bf16[16,128,128]{2,1,0:T(8,128)(2,1)}), bf16[16,128,128]{2,1,0:T(8,128)(2,1)S(1)}, u32[]{:S(2)}, u32[]{:S(2)}) async-start(bf16[16,128,128]{2,1,0:T(8,128)(2,1)} %gather.1), calls=%async_computation.2 | async-start | bytes 1048576 | tf_op jit(solution)/shard_map/all_to_all | solution.py:23

commit v2 on v1

v2 whole, which is shorter than its diff:
```python
import jax
import jax.numpy as jnp
from jax import lax
from jax.experimental import pallas as pl
from jax.experimental.pallas import tpu as pltpu
from jax.sharding import PartitionSpec as P


SB = 128
PB = 128
TAIL = 103
LIMIT = 4 * 1024 * 1024
LOG2E = 1.4426950408889634
FULL = 32000.0
HIGH = 16000.0
VMEM = pltpu.VMEM
SMEM = pltpu.SMEM


def spec(space):
    return pl.BlockSpec(memory_space=space)


def exchange(x, axis):
    return lax.all_to_all(x, axis, split_axis=0, concat_axis=0, tiled=True)


def partial_kernel(pb, sb, cnt, sec, hold, out, inv):
    slots = hold.shape[0]
    nsb = sec.shape[0] // SB
    npb = slots // nsb
    for t in range(slots):
        inv[pb[t] * nsb + sb[t]] = t
    for p in range(npb):
        acc = None
        for s in range(nsb):
            t = inv[p * nsb + s]
            live = (t < cnt[0]).astype(jnp.float32)
            term = live * jnp.dot(hold[t], sec[s * SB : (s + 1) * SB, :], preferred_element_type=jnp.float32)
            acc = term if acc is None else acc + term
        out[p * PB : (p + 1) * PB, :] = acc


def exponent(peak):
    return jnp.floor(jnp.log(jnp.maximum(peak, 1e-30)) * LOG2E + 1.02)


def codes_kernel(pb, sb, days, own, other, codes, meta, mine, wide, flat, turned):
    width = own.shape[1]
    half = codes.shape[1]
    nsb = own.shape[0] // SB
    k = lax.axis_index("day")
    q = lax.axis_index("sec")
    core = k % 2
    first = (k - core) * width
    row = q * mine.shape[0]
    near = pl.ds(pl.multiple_of((row // PB) * PB, PB), PB)
    count = days.shape[1]
    one = jnp.int32(1)
    i8 = lax.broadcasted_iota(jnp.int32, (8, count), 0)
    bits = jnp.zeros((8, count), jnp.int32)
    for j in range(0, TAIL, 8):
        n = min(8, TAIL - j)
        here = days[j : j + n, :] - first
        inside = (here >= 0) & (here < 2 * width)
        word = jnp.where(inside, here & 7, 8)
        bit = lax.shift_left(jnp.full((n, count), one), jnp.where(inside, here >> 3, 0))
        for r in range(n):
            bits = bits | jnp.where(i8 == word[r : r + 1], bit[r : r + 1], 0)
    for b in range(2 * width // 8):
        wide[b * 8 : b * 8 + 8, :] = ((bits >> b) & 1).astype(jnp.float32)
    here = pl.ds(pl.multiple_of(core * width, width), width)
    there = pl.ds(pl.multiple_of((1 - core) * width, width), width)

    def rows(ref):
        parts = [ref[pl.ds(pl.multiple_of(s * SB + core * half, half), half), :] for s in range(nsb)]
        return jnp.concatenate(parts, axis=0)

    found = jnp.dot(rows(own), wide[here, :].astype(jnp.bfloat16), preferred_element_type=jnp.float32)
    found = found + jnp.dot(rows(other), wide[there, :].astype(jnp.bfloat16), preferred_element_type=jnp.float32)
    flat[...] = found
    peak = jnp.max(jnp.max(jnp.abs(found), axis=0, keepdims=True), axis=1, keepdims=True)
    power = exponent(peak)
    meta[...] = jnp.broadcast_to(power, meta.shape)
    scale = jnp.exp2(-power) * FULL
    for t in range(codes.shape[0]):
        part = flat[pl.ds(pl.multiple_of(sb[t] * half, half), half), pl.ds(pl.multiple_of(pb[t] * PB, PB), PB)]
        codes[t] = jnp.round(part * scale).astype(jnp.int32).astype(jnp.int16)
    turned[...] = wide[here, near].T
    mine[...] = turned[pl.ds(pl.multiple_of(row % PB, 8), mine.shape[0]), :]


def share_kernel(arrived, mine, codes, meta, pnl, sent):
    share = jnp.sum(arrived[...], axis=0)
    pnl[...] = share.astype(jnp.bfloat16)
    picked = jnp.sum(share * mine[...], axis=1, keepdims=True)
    shape = share.shape
    rows = lax.broadcasted_iota(jnp.int32, shape, 0)
    diag = rows == lax.broadcasted_iota(jnp.int32, shape, 1)
    line = jnp.sum(jnp.where(diag, picked, 0.0), axis=0, keepdims=True)
    power = exponent(jnp.max(jnp.abs(line), axis=1, keepdims=True))
    scaled = line * jnp.exp2(-power) * HIGH
    high = jnp.round(scaled)
    low = jnp.round((scaled - high) * FULL)
    extra = jnp.where(rows == 0, high, jnp.where(rows == 1, low, jnp.where(rows == 2, power, meta[...])))
    extra = extra.astype(jnp.int32).astype(jnp.int16)
    half = codes.shape[1]
    for k in range(sent.shape[0]):
        sent[k, :half, :] = codes[k]
        sent[k, half:, :] = extra


def tail_kernel(cnt, arrived, out, short):
    half = SB // 2
    sides = [None, None]
    total = None
    for k in range(arrived.shape[0]):
        extra = arrived[k, half:, :].astype(jnp.int32).astype(jnp.float32)
        scale = jnp.exp2(extra[3:4]) / FULL
        part = arrived[k, :half, :].astype(jnp.int32).astype(jnp.float32) * scale
        sides[k % 2] = part if sides[k % 2] is None else sides[k % 2] + part
        line = (extra[0:1] + extra[1:2] / FULL) * (jnp.exp2(extra[2:3]) / HIGH)
        total = line if total is None else total + line
    live = (lax.axis_index("day") < cnt[0]).astype(jnp.float32)
    out[0] = jnp.concatenate(sides, axis=0).T * live / TAIL
    short[...] = (-total / TAIL)[:, : short.shape[1]]


def call(kernel, outs, ins, scratch=(), limit=LIMIT, flops=10**7, moved=600000):
    several = isinstance(outs, tuple)
    return pl.pallas_call(
        kernel,
        out_shape=outs,
        in_specs=[spec(i) for i in ins],
        out_specs=tuple(spec(VMEM) for _ in outs) if several else spec(VMEM),
        scratch_shapes=list(scratch),
        cost_estimate=pl.CostEstimate(flops=flops, bytes_accessed=moved, transcendentals=0),
        compiler_params=pltpu.CompilerParams(vmem_limit_bytes=limit),
    )


def step(sec_pnl, holdings, tile_pblock, tile_sblock, tile_count, tail_days):
    n_day = lax.axis_size("day")
    n_sec = lax.axis_size("sec")
    width = sec_pnl.shape[1]
    slots = holdings.shape[0]
    portfolios = tail_days.shape[0]
    rows = portfolios // n_sec
    half = SB // 2
    f32 = jnp.float32
    shape = jax.ShapeDtypeStruct
    partial = call(
        partial_kernel,
        shape((portfolios, width), f32),
        [SMEM] * 3 + [VMEM] * 2,
        [pltpu.SMEM((slots,), jnp.int32)],
        limit=None,
    )(tile_pblock, tile_sblock, tile_count, sec_pnl, holdings)
    arrived = exchange(partial.reshape(n_sec, rows, width), "sec")
    other = lax.ppermute(sec_pnl, "day", [(i, i ^ 1) for i in range(n_day)])
    codes, meta, mine = call(
        codes_kernel,
        (shape((slots, half, PB), jnp.int16), shape((8, PB), f32), shape((rows, width), f32)),
        [SMEM] * 2 + [VMEM] * 3,
        [
            pltpu.VMEM((2 * width, portfolios), f32),
            pltpu.VMEM((sec_pnl.shape[0] // 2, portfolios), f32),
            pltpu.VMEM((PB, width), f32),
        ],
    )(tile_pblock, tile_sblock, tail_days.T, sec_pnl, other)
    pnl, sent = call(
        share_kernel, (shape((rows, width), jnp.bfloat16), shape((n_day, half + 8, PB), jnp.int16)), [VMEM] * 4
    )(arrived, mine, codes, meta)
    back = exchange(sent, "day")
    tail_mean, short = call(
        tail_kernel, (shape((1, PB, SB), f32), shape((1, rows), f32)), [SMEM, VMEM]
    )(tile_count, back)
    return pnl, short.reshape(rows), tail_mean


def solution(mesh):
    placed = (P("sec", "day"), P("sec", None, None), P("sec"), P("sec"), P("sec"), P())
    return jax.shard_map(
        step,
        mesh=mesh,
        in_specs=placed,
        out_specs=(P("sec", "day"), P("sec"), P(("sec", "day"), None, None)),
        check_vma=False,
    )
```

time: 67.5 us -> 51.9 us (0.77)
  blocking collectives: 0 us -> 24.5 us
  waiting for transfers between devices: 30.3 us -> 7.26 us
  starting transfers between devices: 27 us -> 13.2 us
  local copies, waits for them, and re-layouts: 2 us -> 0.64 us
  Pallas kernels: 5.75 us -> 4.73 us
    all_to_all x0 -> x1, blocking collectives: none -> 24.5 us  [exchange(): return lax.all_to_all(x, axis, split_axis=0, concat_axis=0, tiled=True)]
    all_to_all x3 -> x1, waiting for transfers between devices: 30.3 us -> 7.26 us  [exchange(): return lax.all_to_all(x, axis, split_axis=0, concat_axis=0, tiled=True)]
    all_to_all x3 -> x1, starting transfers between devices: 27 us -> 4.46 us  [exchange(): return lax.all_to_all(x, axis, split_axis=0, concat_axis=0, tiled=True)]
    ppermute x0 -> x1, starting transfers between devices: none -> 8.75 us  [step(): other = lax.ppermute(sec_pnl, 'day', [(i, i ^ 1) for i in range(n_day)])]
    unnamed x12 -> x8, local copies, waits for them, and re-layouts: 2 us -> 0.64 us
    pallas_call x5 -> x4, Pallas kernels: 5.75 us -> 4.73 us  [the longest x1 2.12 us: step(): call(partial_kernel, shape((portfolios, width), f32), [SMEM] * 3 + [VMEM]...]
  transfers between devices with their start and end apart: 3 -> 2, of which waited for: 3 -> 1; matrix products, arithmetic and copies ran while one was open for 1% -> 0% of each run, Pallas kernels for 4% -> 6%
where the time goes in v2:
time: 51.9 us; the launch traced here: 51.7 us
  blocking collectives  24.5 us (47%)
  starting transfers between devices  13.2 us (25%)
  waiting for transfers between devices  7.26 us (14%)
  Pallas kernels  4.73 us (9%)
  between operations  1.35 us (3%)
  local copies, waits for them, and re-layouts  0.64 us (1%)
    all_to_all x1, blocking collectives, exchange(): return lax.all_to_all(x, axis, split_axis=0, concat_axis=0, tiled=True)  24.5 us
    ppermute x1, starting transfers between devices, step(): other = lax.ppermute(sec_pnl, 'day', [(i, i ^ 1) for i in range(n_day)])  8.75 us
    all_to_all x1, waiting for transfers between devices, exchange(): return lax.all_to_all(x, axis, split_axis=0, concat_axis=0, tiled=True)  7.26 us
    all_to_all x1, starting transfers between devices, exchange(): return lax.all_to_all(x, axis, split_axis=0, concat_axis=0, tiled=True)  4.46 us
    pallas_call x1, Pallas kernels, step(): call(partial_kernel, shape((portfolios, width), f32), [SMEM] * 3 + [VMEM]...  2.12 us
    pallas_call x1, Pallas kernels, step(): call(codes_kernel, (shape((slots, half, PB), jnp.int16), shape((8, PB), f...  1.21 us
  transfers between devices with their start and end apart: 2, of which 1 were waited for; matrix products, arithmetic and copies ran while one was open for 0% of the time, Pallas kernels for 6%

profile of v2, /device:TPU:1, one launch (start us, length us, event | category | flops | bytes accessed | tf_op | source)
XLA Modules:
  0.0 51.7 jit_solution(9398119189378375439)
XLA Ops:
  0.6 8.7 %collective-permute-start = (bf16[1024,128]{1,0:T(8,128)(2,1)}, bf16[1024,128]{1,0:T(8,128)(2,1)S(1)}, u32[]{:S(2)}, u32[]{:S(2)}) collective-permute-start(bf16[1024,128]{1,0:T(8,128)(2,1)} %own.1), channel_id=1, source_target_pairs={{0,1},{1,0},{2,3},{3,2},{4,5},{5,4},{6,7},{7,6},{8,9},{9,8},{10,11... | collective-permute-start | bytes 786440 | tf_op jit(solution)/shard_map/ppermute | solution.py:160
  10.0 0.0 copy-start.1
  10.0 2.1 %shard_map.85 = f32[256,128]{1,0:T(8,128)} custom-call(s32[16]{0:T(128)} %pb.3, s32[16]{0:T(128)} %sb.3, s32[1]{0:T(128)S(6)} %copy.9.cnt, bf16[1024,128]{1,0:T(8,128)(2,1)} %own.1, bf16[16,128,128]{2,1,0:T(8,128)(2,1)} %hold.1), custom_call_target="tpu_custom_call" | custom-call | flops 10000000 | bytes 600000 | tf_op jit(solution)/shard_map/pallas_call | solution.py:152
  12.2 0.0 copy-start
  12.2 4.5 %all-to-all-start = ((f32[32,8,128]{2,1,0:T(8,128)}), f32[32,8,128]{2,1,0:T(8,128)S(1)}, u32[]{:S(2)}, u32[]{:S(2)}) async-start(f32[32,8,128]{2,1,0:T(8,128)} %bitcast.4), calls=%async_computation | async-start | bytes 262144 | tf_op jit(solution)/shard_map/all_to_all | solution.py:25
  16.6 0.0 copy-start.2
  16.6 0.0 copy-start.3
  16.7 0.0 collective-permute-done.other
  16.7 0.0 copy-done.1
  16.7 0.0 copy-done
  16.7 0.6 %copy-done.2 = s32[16]{0:T(128)S(1)} copy-done((s32[16]{0:T(128)S(1)}, s32[16]{0:T(128)}, u32[]{:S(2)}) %copy-start.2) | copy-done | bytes 88
  17.3 0.0 copy-done.3
  17.3 1.2 %shard_map.86 = (s16[16,64,128]{2,1,0:T(8,128)(2,1)S(1)}, f32[8,128]{1,0:T(8,128)S(1)}, f32[8,128]{1,0:T(8,128)S(1)}) custom-call(s32[16]{0:T(128)S(1)} %copy-done.2, s32[16]{0:T(128)S(1)} %copy-done.3, s32[103,256]{1,0:T(8,128)S(1)} %bitcast.3, bf16[1024,128]{1,0:T(8,128)(2,1)S(1)} %copy-done, bf16[1024,128]{1,0:T(8,128)(2,1)S(1)} %collective-permute-done.other), custom_call_target="tpu_custom_call" | custom-call | flops 10000000 | bytes 600000 | tf_op jit(solution)/shard_map/pallas_call | solution.py:161
  18.5 7.3 %all-to-all-done.arrived = f32[32,8,128]{2,1,0:T(8,128)S(1)} async-done(((f32[32,8,128]{2,1,0:T(8,128)}), f32[32,8,128]{2,1,0:T(8,128)S(1)}, u32[]{:S(2)}, u32[]{:S(2)}) %all-to-all-start) | async-done | bytes 131104 | tf_op jit(solution)/shard_map/all_to_all | solution.py:25
  25.8 0.6 %shard_map.87 = (bf16[8,128]{1,0:T(8,128)(2,1)}, s16[16,72,128]{2,1,0:T(8,128)(2,1)S(1)}) custom-call(f32[32,8,128]{2,1,0:T(8,128)S(1)} %all-to-all-done.arrived, f32[8,128]{1,0:T(8,128)S(1)} %get-tuple-element.10.mine, s16[16,64,128]{2,1,0:T(8,128)(2,1)S(1)} %get-tuple-element.11.codes, f32[8,128]{1,0:T(8,128)S(1)} %get-tuple-element.12.meta), custom_call_target="tpu_custom_call" | custom-call | flops 10000000 | bytes 600000 | tf_op jit(solution)/shard_map/pallas_call | solution.py:171
  26.4 24.5 %all_to_all.10.arrived = s16[16,72,128]{2,1,0:T(8,128)(2,1)S(1)} all-to-all(s16[16,72,128]{2,1,0:T(8,128)(2,1)S(1)} %get-tuple-element.14), channel_id=1, replica_groups=mesh['sec'=32,'day'=16] {'day'}, dimensions={0} | all-to-all | bytes 589824 | tf_op jit(solution)/shard_map/all_to_all | solution.py:25
  50.9 0.8 %shard_map.88 = (f32[1,128,128]{2,1,0:T(8,128)}, f32[1,8]{1,0:T(1,128)}) custom-call(s32[1]{0:T(128)S(6)} %copy.9.cnt, s16[16,72,128]{2,1,0:T(8,128)(2,1)S(1)} %all_to_all.10.arrived), custom_call_target="tpu_custom_call" | custom-call | flops 10000000 | bytes 600000 | tf_op jit(solution)/shard_map/pallas_call | solution.py:175
Async XLA Ops:
  0.6 16.0 %collective-permute-start = (bf16[1024,128]{1,0:T(8,128)(2,1)}, bf16[1024,128]{1,0:T(8,128)(2,1)S(1)}, u32[]{:S(2)}, u32[]{:S(2)}) collective-permute-start(bf16[1024,128]{1,0:T(8,128)(2,1)} %own.1), channel_id=1, source_target_pairs={{0,1},{1,0},{2,3},{3,2},{4,5},{5,4},{6,7},{7,6},{8,9},{9,8},{10,11... | collective-permute-start | bytes 786440 | tf_op jit(solution)/shard_map/ppermute | solution.py:160
  10.0 6.6 %copy-start.1 = (s32[256,103]{0,1:T(8,128)S(1)}, s32[256,103]{0,1:T(8,128)}, u32[]{:S(2)}) copy-start(s32[256,103]{0,1:T(8,128)} %param.11) | copy-start | bytes 316420
  12.2 4.5 %copy-start = (bf16[1024,128]{1,0:T(8,128)(2,1)S(1)}, bf16[1024,128]{1,0:T(8,128)(2,1)}, u32[]{:S(2)}) copy-start(bf16[1024,128]{1,0:T(8,128)(2,1)} %own.1) | copy-start | bytes 786436
  12.2 13.6 %all-to-all-start = ((f32[32,8,128]{2,1,0:T(8,128)}), f32[32,8,128]{2,1,0:T(8,128)S(1)}, u32[]{:S(2)}, u32[]{:S(2)}) async-start(f32[32,8,128]{2,1,0:T(8,128)} %bitcast.4), calls=%async_computation | async-start | bytes 262144 | tf_op jit(solution)/shard_map/all_to_all | solution.py:25
  16.6 0.7 %copy-start.2 = (s32[16]{0:T(128)S(1)}, s32[16]{0:T(128)}, u32[]{:S(2)}) copy-start(s32[16]{0:T(128)} %pb.3) | copy-start | bytes 196
  16.6 0.7 %copy-start.3 = (s32[16]{0:T(128)S(1)}, s32[16]{0:T(128)}, u32[]{:S(2)}) copy-start(s32[16]{0:T(128)} %sb.3) | copy-start | bytes 196

commit v3 on v2

v3 whole, which is shorter than its diff:
```python
import jax
import jax.numpy as jnp
from jax import lax
from jax.experimental import pallas as pl
from jax.experimental.pallas import tpu as pltpu
from jax.sharding import PartitionSpec as P


SB = 128
PB = 128
TAIL = 103
TEAM = 4
LIMIT = 4 * 1024 * 1024
LOG2E = 1.4426950408889634
FULL = 32000.0
HIGH = 16000.0
VMEM = pltpu.VMEM
SMEM = pltpu.SMEM


def spec(space):
    return pl.BlockSpec(memory_space=space)


def exchange(x, axis):
    return lax.all_to_all(x, axis, split_axis=0, concat_axis=0, tiled=True)


def partial_kernel(pb, sb, cnt, sec, hold, out, inv):
    slots = hold.shape[0]
    nsb = sec.shape[0] // SB
    npb = slots // nsb
    for t in range(slots):
        inv[pb[t] * nsb + sb[t]] = t
    for p in range(npb):
        acc = None
        for s in range(nsb):
            t = inv[p * nsb + s]
            live = (t < cnt[...]).astype(jnp.float32)
            term = live * jnp.dot(hold[t], sec[s * SB : (s + 1) * SB, :], preferred_element_type=jnp.float32)
            acc = term if acc is None else acc + term
        out[p * PB : (p + 1) * PB, :] = acc


def exponent(peak):
    return jnp.floor(jnp.log(jnp.maximum(peak, 1e-30)) * LOG2E + 1.02)


def pack_kernel(sec, *outs):
    part = SB // TEAM
    seat = lax.axis_index("day") % TEAM
    for j, out in enumerate(outs):
        at = (seat ^ (j + 1)) * part
        for s in range(sec.shape[0] // SB):
            out[s * part : (s + 1) * part, :] = sec[pl.ds(pl.multiple_of(s * SB + at, part), part), :]


def codes_kernel(pb, sb, days, own, *refs):
    others = refs[: TEAM - 1]
    codes, meta, mine, wide, flat, turned = refs[TEAM - 1 :]
    width = own.shape[1]
    part = codes.shape[1]
    nsb = own.shape[0] // SB
    k = lax.axis_index("day")
    q = lax.axis_index("sec")
    seat = k % TEAM
    first = (k - seat) * width
    row = q * mine.shape[0]
    near = pl.ds(pl.multiple_of((row // PB) * PB, PB), PB)
    count = days.shape[1]
    deep = TEAM * width // 32
    one = jnp.int32(1)
    at = lax.broadcasted_iota(jnp.int32, (deep, count), 0)
    bits = jnp.zeros((deep, count), jnp.int32)
    for j in range(0, TAIL, 8):
        n = min(8, TAIL - j)
        here = days[j : j + n, :] - first
        inside = (here >= 0) & (here < TEAM * width)
        word = jnp.where(inside, here & (deep - 1), deep)
        bit = lax.shift_left(jnp.full((n, count), one), jnp.where(inside, here // deep, 0))
        for r in range(n):
            bits = bits | jnp.where(at == word[r : r + 1], bit[r : r + 1], 0)
    for b in range(32):
        wide[b * deep : (b + 1) * deep, :] = ((bits >> b) & 1).astype(jnp.float32)

    def span(member):
        return pl.ds(pl.multiple_of(member * width, width), width)

    rows = [own[pl.ds(pl.multiple_of(s * SB + seat * part, part), part), :] for s in range(nsb)]
    rows = [jnp.concatenate(rows, axis=0)] + [other[...] for other in others]
    found = None
    for j in range(TEAM):
        term = jnp.dot(rows[j], wide[span(seat ^ j), :].astype(jnp.bfloat16), preferred_element_type=jnp.float32)
        found = term if found is None else found + term
    flat[...] = found
    peak = jnp.max(jnp.max(jnp.abs(found), axis=0, keepdims=True), axis=1, keepdims=True)
    power = exponent(peak)
    meta[...] = jnp.broadcast_to(power, meta.shape)
    scale = jnp.exp2(-power) * FULL
    for t in range(codes.shape[0]):
        tile = flat[pl.ds(pl.multiple_of(sb[t] * part, part), part), pl.ds(pl.multiple_of(pb[t] * PB, PB), PB)]
        codes[t] = jnp.round(tile * scale).astype(jnp.int32).astype(jnp.int16)
    turned[...] = wide[span(seat), near].T
    mine[...] = turned[pl.ds(pl.multiple_of(row % PB, 8), mine.shape[0]), :]


def share_kernel(arrived, mine, codes, meta, pnl, sent):
    share = jnp.sum(arrived[...], axis=0)
    pnl[...] = share.astype(jnp.bfloat16)
    picked = jnp.sum(share * mine[...], axis=1, keepdims=True)
    shape = share.shape
    rows = lax.broadcasted_iota(jnp.int32, shape, 0)
    diag = rows == lax.broadcasted_iota(jnp.int32, shape, 1)
    line = jnp.sum(jnp.where(diag, picked, 0.0), axis=0, keepdims=True)
    power = exponent(jnp.max(jnp.abs(line), axis=1, keepdims=True))
    scaled = line * jnp.exp2(-power) * HIGH
    high = jnp.round(scaled)
    low = jnp.round((scaled - high) * FULL)
    extra = jnp.where(rows == 0, high, jnp.where(rows == 1, low, jnp.where(rows == 2, power, meta[...])))
    extra = extra.astype(jnp.int32).astype(jnp.int16)
    part = codes.shape[1]
    for k in range(sent.shape[0]):
        sent[k, :part, :] = codes[k]
        sent[k, part:, :] = extra


def tail_kernel(cnt, arrived, out, short):
    part = SB // TEAM
    sides = [None] * TEAM
    total = None
    for k in range(arrived.shape[0]):
        extra = arrived[k, part:, :].astype(jnp.int32).astype(jnp.float32)
        scale = jnp.exp2(extra[3:4]) / FULL
        here = arrived[k, :part, :].astype(jnp.int32).astype(jnp.float32) * scale
        sides[k % TEAM] = here if sides[k % TEAM] is None else sides[k % TEAM] + here
        line = (extra[0:1] + extra[1:2] / FULL) * (jnp.exp2(extra[2:3]) / HIGH)
        total = line if total is None else total + line
    live = (lax.axis_index("day") < cnt[...]).astype(jnp.float32)
    out[0] = jnp.concatenate(sides, axis=0).T * live / TAIL
    short[...] = (-total / TAIL)[:, : short.shape[1]]


def call(kernel, outs, ins, scratch=(), limit=LIMIT, flops=10**7, moved=600000):
    several = isinstance(outs, tuple)
    return pl.pallas_call(
        kernel,
        out_shape=outs,
        in_specs=[spec(i) for i in ins],
        out_specs=tuple(spec(VMEM) for _ in outs) if several else spec(VMEM),
        scratch_shapes=list(scratch),
        cost_estimate=pl.CostEstimate(flops=flops, bytes_accessed=moved, transcendentals=0),
        compiler_params=pltpu.CompilerParams(vmem_limit_bytes=limit),
    )


def step(sec_pnl, holdings, tile_pblock, tile_sblock, tile_count, tail_days):
    n_day = lax.axis_size("day")
    n_sec = lax.axis_size("sec")
    width = sec_pnl.shape[1]
    slots = holdings.shape[0]
    portfolios = tail_days.shape[0]
    rows = portfolios // n_sec
    part = SB // TEAM
    f32 = jnp.float32
    shape = jax.ShapeDtypeStruct
    count = tile_count.reshape(1, 1)
    partial = call(
        partial_kernel,
        shape((portfolios, width), f32),
        [SMEM] * 2 + [VMEM] * 3,
        [pltpu.SMEM((slots,), jnp.int32)],
        limit=None,
    )(tile_pblock, tile_sblock, count, sec_pnl, holdings)
    arrived = exchange(partial.reshape(n_sec, rows, width), "sec")
    packs = call(
        pack_kernel, tuple(shape((sec_pnl.shape[0] // TEAM, width), sec_pnl.dtype) for _ in range(TEAM - 1)), [VMEM]
    )(sec_pnl)
    others = [None] * (TEAM - 1)
    for j in (3, 2, 1):
        others[j - 1] = lax.ppermute(packs[j - 1], "day", [(i, i ^ j) for i in range(n_day)])
    codes, meta, mine = call(
        codes_kernel,
        (shape((slots, part, PB), jnp.int16), shape((8, PB), f32), shape((rows, width), f32)),
        [SMEM] * 2 + [VMEM] * (TEAM + 1),
        [
            pltpu.VMEM((TEAM * width, portfolios), f32),
            pltpu.VMEM((sec_pnl.shape[0] // TEAM, portfolios), f32),
            pltpu.VMEM((PB, width), f32),
        ],
    )(tile_pblock, tile_sblock, tail_days.T, sec_pnl, *others)
    pnl, sent = call(
        share_kernel, (shape((rows, width), jnp.bfloat16), shape((n_day, part + 8, PB), jnp.int16)), [VMEM] * 4
    )(arrived, mine, codes, meta)
    back = exchange(sent, "day")
    tail_mean, short = call(tail_kernel, (shape((1, PB, SB), f32), shape((1, rows), f32)), [VMEM] * 2)(count, back)
    return pnl, short.reshape(rows), tail_mean


def solution(mesh):
    placed = (P("sec", "day"), P("sec", None, None), P("sec"), P("sec"), P("sec"), P())
    return jax.shard_map(
        step,
        mesh=mesh,
        in_specs=placed,
        out_specs=(P("sec", "day"), P("sec"), P(("sec", "day"), None, None)),
        check_vma=False,
    )
```

time: 51.9 us -> 48.9 us (0.942)
  starting transfers between devices: 13.2 us -> 19.4 us
  blocking collectives: 24.5 us -> 19 us
  waiting for transfers between devices: 7.26 us -> 3.96 us
  local copies, waits for them, and re-layouts: 0.64 us -> 0.02 us
    all_to_all x1, waiting for transfers between devices: 7.26 us -> 0.01 us  [exchange(): return lax.all_to_all(x, axis, split_axis=0, concat_axis=0, tiled=True)]
    all_to_all x1, starting transfers between devices: 4.46 us -> 10.6 us  [exchange(): return lax.all_to_all(x, axis, split_axis=0, concat_axis=0, tiled=True)]
    all_to_all x1, blocking collectives: 24.5 us -> 19 us  [exchange(): return lax.all_to_all(x, axis, split_axis=0, concat_axis=0, tiled=True)]
    ppermute x1 -> x3, waiting for transfers between devices: 0.01 us -> 3.95 us  [step(): lax.ppermute(packs[j - 1], 'day', [(i, i ^ j) for i in range(n_day)])]
    unnamed x8, local copies, waits for them, and re-layouts: 0.64 us -> 0.02 us
    pallas_call x4 -> x5, Pallas kernels: 4.73 us -> 4.84 us  [the longest x1 2.1 us: step(): call(partial_kernel, shape((portfolios, width), f32), [SMEM] * 2 + [VMEM]...]
    ppermute x1 -> x3, starting transfers between devices: 8.75 us -> 8.78 us  [step(): lax.ppermute(packs[j - 1], 'day', [(i, i ^ j) for i in range(n_day)])]
  transfers between devices with their start and end apart: 2 -> 4, of which waited for: 1 -> 2; matrix products, arithmetic and copies ran while one was open for 0% -> 0% of each run, Pallas kernels for 6% -> 3%
where the time goes in v3:
time: 48.9 us; the launch traced here: 48.6 us
  starting transfers between devices  19.4 us (40%)
  blocking collectives  19 us (39%)
  Pallas kernels  4.84 us (10%)
  waiting for transfers between devices  3.96 us (8%)
  between operations  1.38 us (3%)
    all_to_all x1, blocking collectives, exchange(): return lax.all_to_all(x, axis, split_axis=0, concat_axis=0, tiled=True)  19 us
    all_to_all x1, starting transfers between devices, exchange(): return lax.all_to_all(x, axis, split_axis=0, concat_axis=0, tiled=True)  10.6 us
    ppermute x3, starting transfers between devices, step(): lax.ppermute(packs[j - 1], 'day', [(i, i ^ j) for i in range(n_day)])  8.78 us
    ppermute x3, waiting for transfers between devices, step(): lax.ppermute(packs[j - 1], 'day', [(i, i ^ j) for i in range(n_day)])  3.95 us
    pallas_call x1, Pallas kernels, step(): call(partial_kernel, shape((portfolios, width), f32), [SMEM] * 2 + [VMEM]...  2.1 us
    pallas_call x1, Pallas kernels, step(): call(codes_kernel, (shape((slots, part, PB), jnp.int16), shape((8, PB), f...  1.33 us
  transfers between devices with their start and end apart: 4, of which 2 were waited for; matrix products, arithmetic and copies ran while one was open for 0% of the time, Pallas kernels for 3%

profile of v3, /device:TPU:1, one launch (start us, length us, event | category | flops | bytes accessed | tf_op | source)
XLA Modules:
  0.0 48.6 jit_solution(13455105131202638214)
XLA Ops:
  1.3 2.1 %shard_map.85 = f32[256,128]{1,0:T(8,128)} custom-call(s32[16]{0:T(128)} %pb.3, s32[16]{0:T(128)} %sb.3, s32[1,1]{1,0:T(1,128)} %bitcast.4.cnt, bf16[1024,128]{1,0:T(8,128)(2,1)} %own.1, bf16[16,128,128]{2,1,0:T(8,128)(2,1)} %hold.1), custom_call_target="tpu_custom_call" | custom-call | flops 10000000 | bytes 600000 | tf_op jit(solution)/shard_map/pallas_call | solution.py:167
  3.4 0.0 copy-start
  3.4 10.6 %all-to-all-start = ((f32[32,8,128]{2,1,0:T(8,128)}), f32[32,8,128]{2,1,0:T(8,128)S(1)}, u32[]{:S(2)}, u32[]{:S(2)}) async-start(f32[32,8,128]{2,1,0:T(8,128)} %bitcast.7), calls=%async_computation | async-start | bytes 262144 | tf_op jit(solution)/shard_map/all_to_all | solution.py:26
  14.0 0.0 copy-done
  14.0 0.0 copy-start.1
  14.1 2.9 %collective-permute-start = (bf16[256,128]{1,0:T(8,128)(2,1)S(1)}, bf16[256,128]{1,0:T(8,128)(2,1)S(1)}, u32[]{:S(2)}, u32[]{:S(2)}) collective-permute-start(bf16[256,128]{1,0:T(8,128)(2,1)S(1)} %get-tuple-element.13), channel_id=1, source_target_pairs={{0,1},{1,0},{2,3},{3,2},{4,5},{5,4},{6,7},{7,6},{8,9},{9,8},{10,11... | collective-permute-start | bytes 196616 | tf_op jit(solution)/shard_map/ppermute | solution.py:180
  16.9 4.0 %collective-permute-start.1 = (bf16[256,128]{1,0:T(8,128)(2,1)S(1)}, bf16[256,128]{1,0:T(8,128)(2,1)S(1)}, u32[]{:S(2)}, u32[]{:S(2)}) collective-permute-start(bf16[256,128]{1,0:T(8,128)(2,1)S(1)} %get-tuple-element.14), channel_id=1, source_target_pairs={{0,2},{1,3},{2,0},{3,1},{4,6},{5,7},{6,4},{7,5},{8,10},{9,11},{10,... | collective-permute-start | bytes 196616 | tf_op jit(solution)/shard_map/ppermute | solution.py:180
  21.0 0.0 copy-start.2
  21.0 0.0 copy-start.3
  21.0 1.9 %collective-permute-start.2 = (bf16[256,128]{1,0:T(8,128)(2,1)S(1)}, bf16[256,128]{1,0:T(8,128)(2,1)S(1)}, u32[]{:S(2)}, u32[]{:S(2)}) collective-permute-start(bf16[256,128]{1,0:T(8,128)(2,1)S(1)} %get-tuple-element.15), channel_id=1, source_target_pairs={{0,3},{1,2},{2,1},{3,0},{4,7},{5,6},{6,5},{7,4},{8,11},{9,10},{10,... | collective-permute-start | bytes 196616 | tf_op jit(solution)/shard_map/ppermute | solution.py:180
  22.9 0.0 collective-permute-done.refs_0_
  22.9 0.5 collective-permute-done.1.refs_1_
  23.4 3.5 %collective-permute-done.2.refs_2_ = bf16[256,128]{1,0:T(8,128)(2,1)S(1)} collective-permute-done((bf16[256,128]{1,0:T(8,128)(2,1)S(1)}, bf16[256,128]{1,0:T(8,128)(2,1)S(1)}, u32[]{:S(2)}, u32[]{:S(2)}) %collective-permute-start.2) | collective-permute-done | bytes 65568 | tf_op jit(solution)/shard_map/ppermute | solution.py:180
  26.9 0.0 copy-done.1
  26.9 0.0 copy-done.2
  26.9 0.0 copy-done.3
  26.9 1.3 %shard_map.87 = (s16[16,32,128]{2,1,0:T(8,128)(2,1)S(1)}, f32[8,128]{1,0:T(8,128)S(1)}, f32[8,128]{1,0:T(8,128)S(1)}) custom-call(s32[16]{0:T(128)S(1)} %copy-done.2, s32[16]{0:T(128)S(1)} %copy-done.3, s32[103,256]{1,0:T(8,128)S(1)} %bitcast.6, bf16[1024,128]{1,0:T(8,128)(2,1)S(1)} %copy-done, bf16[256,128]{1,0:T(8,128)(2,1)S(1)} %collective-permute-done.refs_0_, ...), custom_call_target="tpu_custom_call" | custom-call | flops 10000000 | bytes 600000 | tf_op jit(solution)/shard_map/pallas_call | solution.py:181
  28.2 0.0 all-to-all-done.arrived
  28.2 0.6 %shard_map.88 = (bf16[8,128]{1,0:T(8,128)(2,1)}, s16[16,40,128]{2,1,0:T(8,128)(2,1)S(1)}) custom-call(f32[32,8,128]{2,1,0:T(8,128)S(1)} %all-to-all-done.arrived, f32[8,128]{1,0:T(8,128)S(1)} %get-tuple-element.16.mine, s16[16,32,128]{2,1,0:T(8,128)(2,1)S(1)} %get-tuple-element.17.codes, f32[8,128]{1,0:T(8,128)S(1)} %get-tuple-element.18.meta), custom_call_target="tpu_custom_call" | custom-call | flops 10000000 | bytes 600000 | tf_op jit(solution)/shard_map/pallas_call | solution.py:191
  28.8 19.0 %all_to_all.10.arrived = s16[16,40,128]{2,1,0:T(8,128)(2,1)S(1)} all-to-all(s16[16,40,128]{2,1,0:T(8,128)(2,1)S(1)} %get-tuple-element.20), channel_id=1, replica_groups=mesh['sec'=32,'day'=16] {'day'}, dimensions={0} | all-to-all | bytes 327680 | tf_op jit(solution)/shard_map/all_to_all | solution.py:26
  47.9 0.8 %shard_map.89 = (f32[1,128,128]{2,1,0:T(8,128)}, f32[1,8]{1,0:T(1,128)}) custom-call(s32[1,1]{1,0:T(1,128)} %bitcast.5.cnt, s16[16,40,128]{2,1,0:T(8,128)(2,1)S(1)} %all_to_all.10.arrived), custom_call_target="tpu_custom_call" | custom-call | flops 10000000 | bytes 600000 | tf_op jit(solution)/shard_map/pallas_call | solution.py:195
  (1 shorter events, 0.0 us)
Async XLA Ops:
  3.4 10.6 %copy-start = (bf16[1024,128]{1,0:T(8,128)(2,1)S(1)}, bf16[1024,128]{1,0:T(8,128)(2,1)}, u32[]{:S(2)}) copy-start(bf16[1024,128]{1,0:T(8,128)(2,1)} %own.1) | copy-start | bytes 786436
  3.4 24.8 %all-to-all-start = ((f32[32,8,128]{2,1,0:T(8,128)}), f32[32,8,128]{2,1,0:T(8,128)S(1)}, u32[]{:S(2)}, u32[]{:S(2)}) async-start(f32[32,8,128]{2,1,0:T(8,128)} %bitcast.7), calls=%async_computation | async-start | bytes 262144 | tf_op jit(solution)/shard_map/all_to_all | solution.py:26
  14.0 12.9 %copy-start.1 = (s32[256,103]{0,1:T(8,128)S(1)}, s32[256,103]{0,1:T(8,128)}, u32[]{:S(2)}) copy-start(s32[256,103]{0,1:T(8,128)} %param.11) | copy-start | bytes 316420
  14.1 8.8 %collective-permute-start = (bf16[256,128]{1,0:T(8,128)(2,1)S(1)}, bf16[256,128]{1,0:T(8,128)(2,1)S(1)}, u32[]{:S(2)}, u32[]{:S(2)}) collective-permute-start(bf16[256,128]{1,0:T(8,128)(2,1)S(1)} %get-tuple-element.13), channel_id=1, source_target_pairs={{0,1},{1,0},{2,3},{3,2},{4,5},{5,4},{6,7},{7,6},{8,9},{9,8},{10,11... | collective-permute-start | bytes 196616 | tf_op jit(solution)/shard_map/ppermute | solution.py:180
  16.9 6.5 %collective-permute-start.1 = (bf16[256,128]{1,0:T(8,128)(2,1)S(1)}, bf16[256,128]{1,0:T(8,128)(2,1)S(1)}, u32[]{:S(2)}, u32[]{:S(2)}) collective-permute-start(bf16[256,128]{1,0:T(8,128)(2,1)S(1)} %get-tuple-element.14), channel_id=1, source_target_pairs={{0,2},{1,3},{2,0},{3,1},{4,6},{5,7},{6,4},{7,5},{8,10},{9,11},{10,... | collective-permute-start | bytes 196616 | tf_op jit(solution)/shard_map/ppermute | solution.py:180
  21.0 5.9 %copy-start.2 = (s32[16]{0:T(128)S(1)}, s32[16]{0:T(128)}, u32[]{:S(2)}) copy-start(s32[16]{0:T(128)} %pb.3) | copy-start | bytes 196
  21.0 5.9 %copy-start.3 = (s32[16]{0:T(128)S(1)}, s32[16]{0:T(128)}, u32[]{:S(2)}) copy-start(s32[16]{0:T(128)} %sb.3) | copy-start | bytes 196
  21.0 5.9 %collective-permute-start.2 = (bf16[256,128]{1,0:T(8,128)(2,1)S(1)}, bf16[256,128]{1,0:T(8,128)(2,1)S(1)}, u32[]{:S(2)}, u32[]{:S(2)}) collective-permute-start(bf16[256,128]{1,0:T(8,128)(2,1)S(1)} %get-tuple-element.15), channel_id=1, source_target_pairs={{0,3},{1,2},{2,1},{3,0},{4,7},{5,6},{6,5},{7,4},{8,11},{9,10},{10,... | collective-permute-start | bytes 196616 | tf_op jit(solution)/shard_map/ppermute | solution.py:180

commit v4 on v3

--- a/solution.py
+++ b/solution.py
@@ -55,14 +55,11 @@
             out[s * part : (s + 1) * part, :] = sec[pl.ds(pl.multiple_of(s * SB + at, part), part), :]
 
 
-def codes_kernel(pb, sb, days, own, *refs):
-    others = refs[: TEAM - 1]
-    codes, meta, mine, wide, flat, turned = refs[TEAM - 1 :]
+def mask_kernel(pb, sb, days, own, wide, base, mine, turned):
     width = own.shape[1]
-    part = codes.shape[1]
-    nsb = own.shape[0] // SB
+    part = SB // TEAM
+    q = lax.axis_index("sec")
     k = lax.axis_index("day")
-    q = lax.axis_index("sec")
     seat = k % TEAM
     first = (k - seat) * width
     row = q * mine.shape[0]
@@ -81,17 +78,24 @@
         for r in range(n):
             bits = bits | jnp.where(at == word[r : r + 1], bit[r : r + 1], 0)
     for b in range(32):
-        wide[b * deep : (b + 1) * deep, :] = ((bits >> b) & 1).astype(jnp.float32)
-
-    def span(member):
-        return pl.ds(pl.multiple_of(member * width, width), width)
-
-    rows = [own[pl.ds(pl.multiple_of(s * SB + seat * part, part), part), :] for s in range(nsb)]
-    rows = [jnp.concatenate(rows, axis=0)] + [other[...] for other in others]
-    found = None
-    for j in range(TEAM):
-        term = jnp.dot(rows[j], wide[span(seat ^ j), :].astype(jnp.bfloat16), preferred_element_type=jnp.float32)
-        found = term if found is None else found + term
+        wide[b * deep : (b + 1) * deep, :] = ((bits >> b) & 1).astype(jnp.float32).astype(jnp.bfloat16)
+    span = pl.ds(pl.multiple_of(seat * width, width), width)
+    rows = [own[pl.ds(pl.multiple_of(s * SB + seat * part, part), part), :] for s in range(own.shape[0] // SB)]
+    base[...] = jnp.dot(jnp.concatenate(rows, axis=0), wide[span, :], preferred_element_type=jnp.float32)
+    turned[...] = wide[span, near].astype(jnp.float32).T
+    mine[...] = turned[pl.ds(pl.multiple_of(row % PB, 8), mine.shape[0]), :]
+
+
+def codes_kernel(pb, sb, wide, base, *refs):
+    others = refs[: TEAM - 1]
+    codes, meta, flat = refs[TEAM - 1 :]
+    part = codes.shape[1]
+    width = wide.shape[0] // TEAM
+    seat = lax.axis_index("day") % TEAM
+    found = base[...]
+    for j in range(1, TEAM):
+        span = pl.ds(pl.multiple_of((seat ^ j) * width, width), width)
+        found = found + jnp.dot(others[j - 1][...], wide[span, :], preferred_element_type=jnp.float32)
     flat[...] = found
     peak = jnp.max(jnp.max(jnp.abs(found), axis=0, keepdims=True), axis=1, keepdims=True)
     power = exponent(peak)
@@ -100,8 +104,6 @@
     for t in range(codes.shape[0]):
         tile = flat[pl.ds(pl.multiple_of(sb[t] * part, part), part), pl.ds(pl.multiple_of(pb[t] * PB, PB), PB)]
         codes[t] = jnp.round(tile * scale).astype(jnp.int32).astype(jnp.int16)
-    turned[...] = wide[span(seat), near].T
-    mine[...] = turned[pl.ds(pl.multiple_of(row % PB, 8), mine.shape[0]), :]
 
 
 def share_kernel(arrived, mine, codes, meta, pnl, sent):
@@ -178,16 +180,19 @@
     others = [None] * (TEAM - 1)
     for j in (3, 2, 1):
         others[j - 1] = lax.ppermute(packs[j - 1], "day", [(i, i ^ j) for i in range(n_day)])
-    codes, meta, mine = call(
+    group = sec_pnl.shape[0] // TEAM
+    wide, base, mine = call(
+        mask_kernel,
+        (shape((TEAM * width, portfolios), jnp.bfloat16), shape((group, portfolios), f32), shape((rows, width), f32)),
+        [SMEM] * 2 + [VMEM] * 2,
+        [pltpu.VMEM((PB, width), f32)],
+    )(tile_pblock, tile_sblock, tail_days.T, sec_pnl)
+    codes, meta = call(
         codes_kernel,
-        (shape((slots, part, PB), jnp.int16), shape((8, PB), f32), shape((rows, width), f32)),
+        (shape((slots, part, PB), jnp.int16), shape((8, PB), f32)),
         [SMEM] * 2 + [VMEM] * (TEAM + 1),
-        [
-            pltpu.VMEM((TEAM * width, portfolios), f32),
-            pltpu.VMEM((sec_pnl.shape[0] // TEAM, portfolios), f32),
-            pltpu.VMEM((PB, width), f32),
-        ],
-    )(tile_pblock, tile_sblock, tail_days.T, sec_pnl, *others)
+        [pltpu.VMEM((group, portfolios), f32)],
+    )(tile_pblock, tile_sblock, wide, base, *others)
     pnl, sent = call(
         share_kernel, (shape((rows, width), jnp.bfloat16), shape((n_day, part + 8, PB), jnp.int16)), [VMEM] * 4
     )(arrived, mine, codes, meta)

time: 48.9 us -> 48.5 us (level)
  waiting for transfers between devices: 3.96 us -> 2.82 us
  Pallas kernels: 4.84 us -> 5.53 us
    ppermute x3, waiting for transfers between devices: 3.95 us -> 2.82 us  [step(): lax.ppermute(packs[j - 1], 'day', [(i, i ^ j) for i in range(n_day)])]
    pallas_call x0 -> x1, Pallas kernels: none -> 1.09 us  [step(): call(mask_kernel, (shape((TEAM * width, portfolios), jnp.bfloat16), shape...]
  transfers between devices with their start and end apart: 4 -> 4, of which waited for: 2 -> 1; matrix products, arithmetic and copies ran while one was open for 0% -> 0% of each run, Pallas kernels for 3% -> 4%
where the time goes in v4:
time: 48.5 us; the launch traced here: 48.2 us
  starting transfers between devices  19.4 us (40%)
  blocking collectives  19 us (39%)
  Pallas kernels  5.53 us (11%)
  waiting for transfers between devices  2.82 us (6%)
  between operations  1.41 us (3%)
    all_to_all x1, blocking collectives, exchange(): return lax.all_to_all(x, axis, split_axis=0, concat_axis=0, tiled=True)  19 us
    all_to_all x1, starting transfers between devices, exchange(): return lax.all_to_all(x, axis, split_axis=0, concat_axis=0, tiled=True)  10.6 us
    ppermute x3, starting transfers between devices, step(): lax.ppermute(packs[j - 1], 'day', [(i, i ^ j) for i in range(n_day)])  8.78 us
    ppermute x3, waiting for transfers between devices, step(): lax.ppermute(packs[j - 1], 'day', [(i, i ^ j) for i in range(n_day)])  2.82 us
    pallas_call x1, Pallas kernels, step(): call(partial_kernel, shape((portfolios, width), f32), [SMEM] * 2 + [VMEM]...  2.1 us
    pallas_call x1, Pallas kernels, step(): call(mask_kernel, (shape((TEAM * width, portfolios), jnp.bfloat16), shape...  1.09 us
  transfers between devices with their start and end apart: 4, of which 1 were waited for; matrix products, arithmetic and copies ran while one was open for 0% of the time, Pallas kernels for 4%

profile of v4, /device:TPU:1, one launch (start us, length us, event | category | flops | bytes accessed | tf_op | source)
XLA Modules:
  0.0 48.2 jit_solution(13534639400745578036)
XLA Ops:
  1.3 2.1 %shard_map.85 = f32[256,128]{1,0:T(8,128)} custom-call(s32[16]{0:T(128)} %pb.5, s32[16]{0:T(128)} %sb.5, s32[1,1]{1,0:T(1,128)} %bitcast.4.cnt, bf16[1024,128]{1,0:T(8,128)(2,1)} %sec.3, bf16[16,128,128]{2,1,0:T(8,128)(2,1)} %hold.1), custom_call_target="tpu_custom_call" | custom-call | flops 10000000 | bytes 600000 | tf_op jit(solution)/shard_map/pallas_call | solution.py:169
  3.4 0.0 copy-start
  3.4 10.6 %all-to-all-start = ((f32[32,8,128]{2,1,0:T(8,128)}), f32[32,8,128]{2,1,0:T(8,128)S(1)}, u32[]{:S(2)}, u32[]{:S(2)}) async-start(f32[32,8,128]{2,1,0:T(8,128)} %bitcast.7), calls=%async_computation | async-start | bytes 262144 | tf_op jit(solution)/shard_map/all_to_all | solution.py:26
  14.0 0.0 copy-done
  14.0 0.0 copy-start.1
  14.1 2.9 %collective-permute-start = (bf16[256,128]{1,0:T(8,128)(2,1)S(1)}, bf16[256,128]{1,0:T(8,128)(2,1)S(1)}, u32[]{:S(2)}, u32[]{:S(2)}) collective-permute-start(bf16[256,128]{1,0:T(8,128)(2,1)S(1)} %get-tuple-element.18), channel_id=1, source_target_pairs={{0,1},{1,0},{2,3},{3,2},{4,5},{5,4},{6,7},{7,6},{8,9},{9,8},{10,11... | collective-permute-start | bytes 196616 | tf_op jit(solution)/shard_map/ppermute | solution.py:182
  16.9 4.0 %collective-permute-start.1 = (bf16[256,128]{1,0:T(8,128)(2,1)S(1)}, bf16[256,128]{1,0:T(8,128)(2,1)S(1)}, u32[]{:S(2)}, u32[]{:S(2)}) collective-permute-start(bf16[256,128]{1,0:T(8,128)(2,1)S(1)} %get-tuple-element.19), channel_id=1, source_target_pairs={{0,2},{1,3},{2,0},{3,1},{4,6},{5,7},{6,4},{7,5},{8,10},{9,11},{10,... | collective-permute-start | bytes 196616 | tf_op jit(solution)/shard_map/ppermute | solution.py:182
  21.0 0.0 copy-start.2
  21.0 0.0 copy-start.3
  21.0 1.9 %collective-permute-start.2 = (bf16[256,128]{1,0:T(8,128)(2,1)S(1)}, bf16[256,128]{1,0:T(8,128)(2,1)S(1)}, u32[]{:S(2)}, u32[]{:S(2)}) collective-permute-start(bf16[256,128]{1,0:T(8,128)(2,1)S(1)} %get-tuple-element.20), channel_id=1, source_target_pairs={{0,3},{1,2},{2,1},{3,0},{4,7},{5,6},{6,5},{7,4},{8,11},{9,10},{10,... | collective-permute-start | bytes 196616 | tf_op jit(solution)/shard_map/ppermute | solution.py:182
  22.9 0.0 copy-done.1
  22.9 0.0 copy-done.2
  22.9 0.0 copy-done.3
  22.9 1.1 %shard_map.86 = (bf16[512,256]{1,0:T(8,128)(2,1)S(1)}, f32[256,256]{1,0:T(8,128)S(1)}, f32[8,128]{1,0:T(8,128)S(1)}) custom-call(s32[16]{0:T(128)S(1)} %copy-done.2, s32[16]{0:T(128)S(1)} %copy-done.3, s32[103,256]{1,0:T(8,128)S(1)} %bitcast.6, bf16[1024,128]{1,0:T(8,128)(2,1)S(1)} %copy-done), custom_call_target="tpu_custom_call" | custom-call | flops 10000000 | bytes 600000 | tf_op jit(solution)/shard_map/pallas_call | solution.py:184
  24.0 0.0 collective-permute-done.refs_0_
  24.0 0.0 collective-permute-done.1.refs_1_
  24.1 2.8 %collective-permute-done.2.refs_2_ = bf16[256,128]{1,0:T(8,128)(2,1)S(1)} collective-permute-done((bf16[256,128]{1,0:T(8,128)(2,1)S(1)}, bf16[256,128]{1,0:T(8,128)(2,1)S(1)}, u32[]{:S(2)}, u32[]{:S(2)}) %collective-permute-start.2) | collective-permute-done | bytes 65568 | tf_op jit(solution)/shard_map/ppermute | solution.py:182
  26.9 0.9 %shard_map.88 = (s16[16,32,128]{2,1,0:T(8,128)(2,1)S(1)}, f32[8,128]{1,0:T(8,128)S(1)}) custom-call(s32[16]{0:T(128)S(1)} %copy-done.2, s32[16]{0:T(128)S(1)} %copy-done.3, bf16[512,256]{1,0:T(8,128)(2,1)S(1)} %get-tuple-element.16.wide, f32[256,256]{1,0:T(8,128)S(1)} %get-tuple-element.17.base, bf16[256,128]{1,0:T(8,128)(2,1)S(1)} %collective-permute-done.refs_0_, ...), custom_call_target="tpu_custom_call" | custom-call | flops 10000000 | bytes 600000 | tf_op jit(solution)/shard_map/pallas_call | solution.py:190
  27.8 0.0 all-to-all-done.arrived
  27.8 0.6 %shard_map.89 = (bf16[8,128]{1,0:T(8,128)(2,1)}, s16[16,40,128]{2,1,0:T(8,128)(2,1)S(1)}) custom-call(f32[32,8,128]{2,1,0:T(8,128)S(1)} %all-to-all-done.arrived, f32[8,128]{1,0:T(8,128)S(1)} %get-tuple-element.15.mine, s16[16,32,128]{2,1,0:T(8,128)(2,1)S(1)} %get-tuple-element.21.codes, f32[8,128]{1,0:T(8,128)S(1)} %get-tuple-element.22.meta), custom_call_target="tpu_custom_call" | custom-call | flops 10000000 | bytes 600000 | tf_op jit(solution)/shard_map/pallas_call | solution.py:196
  28.4 19.0 %all_to_all.10.arrived = s16[16,40,128]{2,1,0:T(8,128)(2,1)S(1)} all-to-all(s16[16,40,128]{2,1,0:T(8,128)(2,1)S(1)} %get-tuple-element.24), channel_id=1, replica_groups=mesh['sec'=32,'day'=16] {'day'}, dimensions={0} | all-to-all | bytes 327680 | tf_op jit(solution)/shard_map/all_to_all | solution.py:26
  47.5 0.8 %shard_map.90 = (f32[1,128,128]{2,1,0:T(8,128)}, f32[1,8]{1,0:T(1,128)}) custom-call(s32[1,1]{1,0:T(1,128)} %bitcast.5.cnt, s16[16,40,128]{2,1,0:T(8,128)(2,1)S(1)} %all_to_all.10.arrived), custom_call_target="tpu_custom_call" | custom-call | flops 10000000 | bytes 600000 | tf_op jit(solution)/shard_map/pallas_call | solution.py:200
  (1 shorter events, 0.0 us)
Async XLA Ops:
  3.4 10.6 %copy-start = (bf16[1024,128]{1,0:T(8,128)(2,1)S(1)}, bf16[1024,128]{1,0:T(8,128)(2,1)}, u32[]{:S(2)}) copy-start(bf16[1024,128]{1,0:T(8,128)(2,1)} %sec.3) | copy-start | bytes 786436
  3.4 24.4 %all-to-all-start = ((f32[32,8,128]{2,1,0:T(8,128)}), f32[32,8,128]{2,1,0:T(8,128)S(1)}, u32[]{:S(2)}, u32[]{:S(2)}) async-start(f32[32,8,128]{2,1,0:T(8,128)} %bitcast.7), calls=%async_computation | async-start | bytes 262144 | tf_op jit(solution)/shard_map/all_to_all | solution.py:26
  14.0 8.9 %copy-start.1 = (s32[256,103]{0,1:T(8,128)S(1)}, s32[256,103]{0,1:T(8,128)}, u32[]{:S(2)}) copy-start(s32[256,103]{0,1:T(8,128)} %param.11) | copy-start | bytes 316420
  14.1 10.0 %collective-permute-start = (bf16[256,128]{1,0:T(8,128)(2,1)S(1)}, bf16[256,128]{1,0:T(8,128)(2,1)S(1)}, u32[]{:S(2)}, u32[]{:S(2)}) collective-permute-start(bf16[256,128]{1,0:T(8,128)(2,1)S(1)} %get-tuple-element.18), channel_id=1, source_target_pairs={{0,1},{1,0},{2,3},{3,2},{4,5},{5,4},{6,7},{7,6},{8,9},{9,8},{10,11... | collective-permute-start | bytes 196616 | tf_op jit(solution)/shard_map/ppermute | solution.py:182
  16.9 7.1 %collective-permute-start.1 = (bf16[256,128]{1,0:T(8,128)(2,1)S(1)}, bf16[256,128]{1,0:T(8,128)(2,1)S(1)}, u32[]{:S(2)}, u32[]{:S(2)}) collective-permute-start(bf16[256,128]{1,0:T(8,128)(2,1)S(1)} %get-tuple-element.19), channel_id=1, source_target_pairs={{0,2},{1,3},{2,0},{3,1},{4,6},{5,7},{6,4},{7,5},{8,10},{9,11},{10,... | collective-permute-start | bytes 196616 | tf_op jit(solution)/shard_map/ppermute | solution.py:182
  21.0 2.0 %copy-start.2 = (s32[16]{0:T(128)S(1)}, s32[16]{0:T(128)}, u32[]{:S(2)}) copy-start(s32[16]{0:T(128)} %pb.5) | copy-start | bytes 196
  21.0 2.0 %copy-start.3 = (s32[16]{0:T(128)S(1)}, s32[16]{0:T(128)}, u32[]{:S(2)}) copy-start(s32[16]{0:T(128)} %sb.5) | copy-start | bytes 196
  21.0 5.9 %collective-permute-start.2 = (bf16[256,128]{1,0:T(8,128)(2,1)S(1)}, bf16[256,128]{1,0:T(8,128)(2,1)S(1)}, u32[]{:S(2)}, u32[]{:S(2)}) collective-permute-start(bf16[256,128]{1,0:T(8,128)(2,1)S(1)} %get-tuple-element.20), channel_id=1, source_target_pairs={{0,3},{1,2},{2,1},{3,0},{4,7},{5,6},{6,5},{7,4},{8,11},{9,10},{10,... | collective-permute-start | bytes 196616 | tf_op jit(solution)/shard_map/ppermute | solution.py:182

commit v5 on v4

--- a/solution.py
+++ b/solution.py
@@ -9,7 +9,10 @@
 SB = 128
 PB = 128
 TAIL = 103
-TEAM = 4
+TEAM = 2
+PER = 8
+SEC_ROOT = 20
+DAY_ROOT = 12
 LIMIT = 4 * 1024 * 1024
 LOG2E = 1.4426950408889634
 FULL = 32000.0
@@ -22,8 +25,13 @@
     return pl.BlockSpec(memory_space=space)
 
 
-def exchange(x, axis):
-    return lax.all_to_all(x, axis, split_axis=0, concat_axis=0, tiled=True)
+def order_of(count, root):
+    return [(root + i) % count for i in range(count)]
+
+
+def exchange(x, axis, root):
+    order = order_of(x.shape[0], root)
+    return lax.all_to_all(x, axis, split_axis=0, concat_axis=0, tiled=True, axis_index_groups=[order])
 
 
 def partial_kernel(pb, sb, cnt, sec, hold, out, inv):
@@ -39,7 +47,9 @@
             live = (t < cnt[...]).astype(jnp.float32)
             term = live * jnp.dot(hold[t], sec[s * SB : (s + 1) * SB, :], preferred_element_type=jnp.float32)
             acc = term if acc is None else acc + term
-        out[p * PB : (p + 1) * PB, :] = acc
+        for i in range(PB // PER):
+            at = ((p * PB // PER + i - SEC_ROOT) % (npb * PB // PER)) * PER
+            out[at : at + PER, :] = acc[i * PER : (i + 1) * PER, :]
 
 
 def exponent(peak):
@@ -86,10 +96,10 @@
     mine[...] = turned[pl.ds(pl.multiple_of(row % PB, 8), mine.shape[0]), :]
 
 
-def codes_kernel(pb, sb, wide, base, *refs):
+def share_kernel(pb, sb, arrived, mine, wide, base, *refs):
     others = refs[: TEAM - 1]
-    codes, meta, flat = refs[TEAM - 1 :]
-    part = codes.shape[1]
+    pnl, sent, flat = refs[TEAM - 1 :]
+    part = SB // TEAM
     width = wide.shape[0] // TEAM
     seat = lax.axis_index("day") % TEAM
     found = base[...]
@@ -98,15 +108,11 @@
         found = found + jnp.dot(others[j - 1][...], wide[span, :], preferred_element_type=jnp.float32)
     flat[...] = found
     peak = jnp.max(jnp.max(jnp.abs(found), axis=0, keepdims=True), axis=1, keepdims=True)
-    power = exponent(peak)
-    meta[...] = jnp.broadcast_to(power, meta.shape)
-    scale = jnp.exp2(-power) * FULL
-    for t in range(codes.shape[0]):
+    held = exponent(peak)
+    scale = jnp.exp2(-held) * FULL
+    for i, t in enumerate(order_of(sent.shape[0], DAY_ROOT)):
         tile = flat[pl.ds(pl.multiple_of(sb[t] * part, part), part), pl.ds(pl.multiple_of(pb[t] * PB, PB), PB)]
-        codes[t] = jnp.round(tile * scale).astype(jnp.int32).astype(jnp.int16)
-
-
-def share_kernel(arrived, mine, codes, meta, pnl, sent):
+        sent[i, :part, :] = jnp.round(tile * scale).astype(jnp.int32).astype(jnp.int16)
     share = jnp.sum(arrived[...], axis=0)
     pnl[...] = share.astype(jnp.bfloat16)
     picked = jnp.sum(share * mine[...], axis=1, keepdims=True)
@@ -118,22 +124,20 @@
     scaled = line * jnp.exp2(-power) * HIGH
     high = jnp.round(scaled)
     low = jnp.round((scaled - high) * FULL)
-    extra = jnp.where(rows == 0, high, jnp.where(rows == 1, low, jnp.where(rows == 2, power, meta[...])))
+    extra = jnp.where(rows == 0, high, jnp.where(rows == 1, low, jnp.where(rows == 2, power, held)))
     extra = extra.astype(jnp.int32).astype(jnp.int16)
-    part = codes.shape[1]
-    for k in range(sent.shape[0]):
-        sent[k, :part, :] = codes[k]
-        sent[k, part:, :] = extra
+    for i in range(sent.shape[0]):
+        sent[i, part:, :] = extra
 
 
 def tail_kernel(cnt, arrived, out, short):
     part = SB // TEAM
     sides = [None] * TEAM
     total = None
-    for k in range(arrived.shape[0]):
-        extra = arrived[k, part:, :].astype(jnp.int32).astype(jnp.float32)
+    for i, k in enumerate(order_of(arrived.shape[0], DAY_ROOT)):
+        extra = arrived[i, part:, :].astype(jnp.int32).astype(jnp.float32)
         scale = jnp.exp2(extra[3:4]) / FULL
-        here = arrived[k, :part, :].astype(jnp.int32).astype(jnp.float32) * scale
+        here = arrived[i, :part, :].astype(jnp.int32).astype(jnp.float32) * scale
         sides[k % TEAM] = here if sides[k % TEAM] is None else sides[k % TEAM] + here
         line = (extra[0:1] + extra[1:2] / FULL) * (jnp.exp2(extra[2:3]) / HIGH)
         total = line if total is None else total + line
@@ -173,12 +177,12 @@
         [pltpu.SMEM((slots,), jnp.int32)],
         limit=None,
     )(tile_pblock, tile_sblock, count, sec_pnl, holdings)
-    arrived = exchange(partial.reshape(n_sec, rows, width), "sec")
+    arrived = exchange(partial.reshape(n_sec, rows, width), "sec", SEC_ROOT)
     packs = call(
         pack_kernel, tuple(shape((sec_pnl.shape[0] // TEAM, width), sec_pnl.dtype) for _ in range(TEAM - 1)), [VMEM]
     )(sec_pnl)
     others = [None] * (TEAM - 1)
-    for j in (3, 2, 1):
+    for j in range(TEAM - 1, 0, -1):
         others[j - 1] = lax.ppermute(packs[j - 1], "day", [(i, i ^ j) for i in range(n_day)])
     group = sec_pnl.shape[0] // TEAM
     wide, base, mine = call(
@@ -187,16 +191,13 @@
         [SMEM] * 2 + [VMEM] * 2,
         [pltpu.VMEM((PB, width), f32)],
     )(tile_pblock, tile_sblock, tail_days.T, sec_pnl)
-    codes, meta = call(
-        codes_kernel,
-        (shape((slots, part, PB), jnp.int16), shape((8, PB), f32)),
-        [SMEM] * 2 + [VMEM] * (TEAM + 1),
+    pnl, sent = call(
+        share_kernel,
+        (shape((rows, width), jnp.bfloat16), shape((n_day, part + 8, PB), jnp.int16)),
+        [SMEM] * 2 + [VMEM] * (TEAM + 3),
         [pltpu.VMEM((group, portfolios), f32)],
-    )(tile_pblock, tile_sblock, wide, base, *others)
-    pnl, sent = call(
-        share_kernel, (shape((rows, width), jnp.bfloat16), shape((n_day, part + 8, PB), jnp.int16)), [VMEM] * 4
-    )(arrived, mine, codes, meta)
-    back = exchange(sent, "day")
+    )(tile_pblock, tile_sblock, arrived, mine, wide, base, *others)
+    back = exchange(sent, "day", DAY_ROOT)
     tail_mean, short = call(tail_kernel, (shape((1, PB, SB), f32), shape((1, rows), f32)), [VMEM] * 2)(count, back)
     return pnl, short.reshape(rows), tail_mean
 

time: 48.5 us -> 43.5 us (0.90)
  waiting for transfers between devices: 2.82 us -> 0.01 us
  blocking collectives: 19 us -> 17.7 us
  starting transfers between devices: 19.4 us -> 18.8 us
    ppermute x3 -> x1, waiting for transfers between devices: 2.82 us -> 0.01 us  [step(): lax.ppermute(packs[j - 1], 'day', [(i, i ^ j) for i in range(n_day)])]
    ppermute x3 -> x1, starting transfers between devices: 8.78 us -> 6.26 us  [step(): lax.ppermute(packs[j - 1], 'day', [(i, i ^ j) for i in range(n_day)])]
    all_to_all x1, starting transfers between devices: 10.6 us -> 12.5 us  [exchange(): lax.all_to_all(x, axis, split_axis=0, concat_axis=0, tiled=True, axis_ind...]
    all_to_all x1, blocking collectives: 19 us -> 17.7 us  [exchange(): lax.all_to_all(x, axis, split_axis=0, concat_axis=0, tiled=True, axis_ind...]
    pallas_call x1 -> x0, Pallas kernels: 0.93 us -> none  [step(): call(codes_kernel, (shape((slots, part, PB), jnp.int16), shape((8, PB), f...]
    pallas_call x1, Pallas kernels: 0.61 us -> 1.36 us  [step(): call(share_kernel, (shape((rows, width), jnp.bfloat16), shape((n_day, par...]
  transfers between devices with their start and end apart: 4 -> 2, of which waited for: 1 -> 0; matrix products, arithmetic and copies ran while one was open for 0% -> 0% of each run, Pallas kernels for 4% -> 2%
where the time goes in v5:
time: 43.5 us; the launch traced here: 43.2 us
  starting transfers between devices  18.8 us (43%)
  blocking collectives  17.7 us (41%)
  Pallas kernels  5.29 us (12%)
  between operations  1.37 us (3%)
    all_to_all x1, blocking collectives, exchange(): lax.all_to_all(x, axis, split_axis=0, concat_axis=0, tiled=True, axis_ind...  17.7 us
    all_to_all x1, starting transfers between devices, exchange(): lax.all_to_all(x, axis, split_axis=0, concat_axis=0, tiled=True, axis_ind...  12.5 us
    ppermute x1, starting transfers between devices, step(): lax.ppermute(packs[j - 1], 'day', [(i, i ^ j) for i in range(n_day)])  6.26 us
    pallas_call x1, Pallas kernels, step(): call(partial_kernel, shape((portfolios, width), f32), [SMEM] * 2 + [VMEM]...  2.1 us
    pallas_call x1, Pallas kernels, step(): call(share_kernel, (shape((rows, width), jnp.bfloat16), shape((n_day, par...  1.36 us
    pallas_call x1, Pallas kernels, step(): call(mask_kernel, (shape((TEAM * width, portfolios), jnp.bfloat16), shape...  1.03 us
  transfers between devices with their start and end apart: 2, of which 0 were waited for; matrix products, arithmetic and copies ran while one was open for 0% of the time, Pallas kernels for 2%

profile of v5, /device:TPU:1, one launch (start us, length us, event | category | flops | bytes accessed | tf_op | source)
XLA Modules:
  0.0 43.2 jit_solution(1041142233901917006)
XLA Ops:
  1.3 2.1 %shard_map.85 = f32[256,128]{1,0:T(8,128)} custom-call(s32[16]{0:T(128)} %pb.5, s32[16]{0:T(128)} %sb.5, s32[1,1]{1,0:T(1,128)} %bitcast.4.cnt, bf16[1024,128]{1,0:T(8,128)(2,1)} %sec.3, bf16[16,128,128]{2,1,0:T(8,128)(2,1)} %hold.1), custom_call_target="tpu_custom_call" | custom-call | flops 10000000 | bytes 600000 | tf_op jit(solution)/shard_map/pallas_call | solution.py:173
  3.4 0.0 copy-start
  3.4 12.5 %all-to-all-start = ((f32[32,8,128]{2,1,0:T(8,128)}), f32[32,8,128]{2,1,0:T(8,128)S(1)}, u32[]{:S(2)}, u32[]{:S(2)}) async-start(f32[32,8,128]{2,1,0:T(8,128)} %bitcast.7), calls=%async_computation | async-start | bytes 262144 | tf_op jit(solution)/shard_map/all_to_all | solution.py:34
  15.9 0.0 copy-done
  15.9 0.0 copy-start.1
  16.0 0.0 copy-start.2
  16.0 0.0 copy-start.3
  16.0 6.3 %collective-permute-start = (bf16[512,128]{1,0:T(8,128)(2,1)S(1)}, bf16[512,128]{1,0:T(8,128)(2,1)S(1)}, u32[]{:S(2)}, u32[]{:S(2)}) collective-permute-start(bf16[512,128]{1,0:T(8,128)(2,1)S(1)} %shard_map.87), channel_id=1, source_target_pairs={{0,1},{1,0},{2,3},{3,2},{4,5},{5,4},{6,7},{7,6},{8,9},{9,8},{10,11... | collective-permute-start | bytes 393224 | tf_op jit(solution)/shard_map/ppermute | solution.py:186
  22.2 0.0 copy-done.1
  22.3 0.0 copy-done.2
  22.3 0.0 copy-done.3
  22.3 1.0 %shard_map.86 = (bf16[256,256]{1,0:T(8,128)(2,1)S(1)}, f32[512,256]{1,0:T(8,128)S(1)}, f32[8,128]{1,0:T(8,128)S(1)}) custom-call(s32[16]{0:T(128)S(1)} %copy-done.2, s32[16]{0:T(128)S(1)} %copy-done.3, s32[103,256]{1,0:T(8,128)S(1)} %bitcast.6, bf16[1024,128]{1,0:T(8,128)(2,1)S(1)} %copy-done), custom_call_target="tpu_custom_call" | custom-call | flops 10000000 | bytes 600000 | tf_op jit(solution)/shard_map/pallas_call | solution.py:188
  23.3 0.0 collective-permute-done.refs_0_
  23.3 0.0 all-to-all-done.arrived
  23.3 1.4 %shard_map.88 = (bf16[8,128]{1,0:T(8,128)(2,1)}, s16[16,72,128]{2,1,0:T(8,128)(2,1)S(1)}) custom-call(s32[16]{0:T(128)S(1)} %copy-done.2, s32[16]{0:T(128)S(1)} %copy-done.3, f32[32,8,128]{2,1,0:T(8,128)S(1)} %all-to-all-done.arrived, f32[8,128]{1,0:T(8,128)S(1)} %get-tuple-element.10.mine, bf16[256,256]{1,0:T(8,128)(2,1)S(1)} %get-tuple-element.11.wide, ...), custom_call_target="tpu_custom_call" | custom-call | flops 10000000 | bytes 600000 | tf_op jit(solution)/shard_map/pallas_call | solution.py:194
  24.7 17.7 %all_to_all.10.arrived = s16[16,72,128]{2,1,0:T(8,128)(2,1)S(1)} all-to-all(s16[16,72,128]{2,1,0:T(8,128)(2,1)S(1)} %get-tuple-element.14), channel_id=1, replica_groups={{12,13,14,15,0,1,2,3,4,5,6,7,8,9,10,11},{28,29,30,31,16,17,18,19,20,21,..., dimensions={0} | all-to-all | bytes 589824 | tf_op jit(solution)/shard_map/all_to_all | solution.py:34
  42.4 0.8 %shard_map.89 = (f32[1,128,128]{2,1,0:T(8,128)}, f32[1,8]{1,0:T(1,128)}) custom-call(s32[1,1]{1,0:T(1,128)} %bitcast.5.cnt, s16[16,72,128]{2,1,0:T(8,128)(2,1)S(1)} %all_to_all.10.arrived), custom_call_target="tpu_custom_call" | custom-call | flops 10000000 | bytes 600000 | tf_op jit(solution)/shard_map/pallas_call | solution.py:201
  (1 shorter events, 0.0 us)
Async XLA Ops:
  3.4 12.5 %copy-start = (bf16[1024,128]{1,0:T(8,128)(2,1)S(1)}, bf16[1024,128]{1,0:T(8,128)(2,1)}, u32[]{:S(2)}) copy-start(bf16[1024,128]{1,0:T(8,128)(2,1)} %sec.3) | copy-start | bytes 786436
  3.4 19.9 %all-to-all-start = ((f32[32,8,128]{2,1,0:T(8,128)}), f32[32,8,128]{2,1,0:T(8,128)S(1)}, u32[]{:S(2)}, u32[]{:S(2)}) async-start(f32[32,8,128]{2,1,0:T(8,128)} %bitcast.7), calls=%async_computation | async-start | bytes 262144 | tf_op jit(solution)/shard_map/all_to_all | solution.py:34
  15.9 6.3 %copy-start.1 = (s32[256,103]{0,1:T(8,128)S(1)}, s32[256,103]{0,1:T(8,128)}, u32[]{:S(2)}) copy-start(s32[256,103]{0,1:T(8,128)} %param.11) | copy-start | bytes 316420
  16.0 6.3 %copy-start.2 = (s32[16]{0:T(128)S(1)}, s32[16]{0:T(128)}, u32[]{:S(2)}) copy-start(s32[16]{0:T(128)} %pb.5) | copy-start | bytes 196
  16.0 6.3 %copy-start.3 = (s32[16]{0:T(128)S(1)}, s32[16]{0:T(128)}, u32[]{:S(2)}) copy-start(s32[16]{0:T(128)} %sb.5) | copy-start | bytes 196
  16.0 7.3 %collective-permute-start = (bf16[512,128]{1,0:T(8,128)(2,1)S(1)}, bf16[512,128]{1,0:T(8,128)(2,1)S(1)}, u32[]{:S(2)}, u32[]{:S(2)}) collective-permute-start(bf16[512,128]{1,0:T(8,128)(2,1)S(1)} %shard_map.87), channel_id=1, source_target_pairs={{0,1},{1,0},{2,3},{3,2},{4,5},{5,4},{6,7},{7,6},{8,9},{9,8},{10,11... | collective-permute-start | bytes 393224 | tf_op jit(solution)/shard_map/ppermute | solution.py:186

commit v6 on v4

--- a/solution.py
+++ b/solution.py
@@ -9,7 +9,10 @@
 SB = 128
 PB = 128
 TAIL = 103
-TEAM = 4
+TEAM = 2
+PER = 8
+SEC_ROOT = 28
+DAY_ROOT = 12
 LIMIT = 4 * 1024 * 1024
 LOG2E = 1.4426950408889634
 FULL = 32000.0
@@ -22,8 +25,13 @@
     return pl.BlockSpec(memory_space=space)
 
 
-def exchange(x, axis):
-    return lax.all_to_all(x, axis, split_axis=0, concat_axis=0, tiled=True)
+def order_of(count, root):
+    return [(root + i) % count for i in range(count)]
+
+
+def exchange(x, axis, root):
+    order = order_of(x.shape[0], root)
+    return lax.all_to_all(x, axis, split_axis=0, concat_axis=0, tiled=True, axis_index_groups=[order])
 
 
 def partial_kernel(pb, sb, cnt, sec, hold, out, inv):
@@ -39,7 +47,9 @@
             live = (t < cnt[...]).astype(jnp.float32)
             term = live * jnp.dot(hold[t], sec[s * SB : (s + 1) * SB, :], preferred_element_type=jnp.float32)
             acc = term if acc is None else acc + term
-        out[p * PB : (p + 1) * PB, :] = acc
+        for i in range(PB // PER):
+            at = ((p * PB // PER + i - SEC_ROOT) % (npb * PB // PER)) * PER
+            out[at : at + PER, :] = acc[i * PER : (i + 1) * PER, :]
 
 
 def exponent(peak):
@@ -121,19 +131,19 @@
     extra = jnp.where(rows == 0, high, jnp.where(rows == 1, low, jnp.where(rows == 2, power, meta[...])))
     extra = extra.astype(jnp.int32).astype(jnp.int16)
     part = codes.shape[1]
-    for k in range(sent.shape[0]):
-        sent[k, :part, :] = codes[k]
-        sent[k, part:, :] = extra
+    for i, k in enumerate(order_of(sent.shape[0], DAY_ROOT)):
+        sent[i, :part, :] = codes[k]
+        sent[i, part:, :] = extra
 
 
 def tail_kernel(cnt, arrived, out, short):
     part = SB // TEAM
     sides = [None] * TEAM
     total = None
-    for k in range(arrived.shape[0]):
-        extra = arrived[k, part:, :].astype(jnp.int32).astype(jnp.float32)
+    for i, k in enumerate(order_of(arrived.shape[0], DAY_ROOT)):
+        extra = arrived[i, part:, :].astype(jnp.int32).astype(jnp.float32)
         scale = jnp.exp2(extra[3:4]) / FULL
-        here = arrived[k, :part, :].astype(jnp.int32).astype(jnp.float32) * scale
+        here = arrived[i, :part, :].astype(jnp.int32).astype(jnp.float32) * scale
         sides[k % TEAM] = here if sides[k % TEAM] is None else sides[k % TEAM] + here
         line = (extra[0:1] + extra[1:2] / FULL) * (jnp.exp2(extra[2:3]) / HIGH)
         total = line if total is None else total + line
@@ -173,12 +183,12 @@
         [pltpu.SMEM((slots,), jnp.int32)],
         limit=None,
     )(tile_pblock, tile_sblock, count, sec_pnl, holdings)
-    arrived = exchange(partial.reshape(n_sec, rows, width), "sec")
+    arrived = exchange(partial.reshape(n_sec, rows, width), "sec", SEC_ROOT)
     packs = call(
         pack_kernel, tuple(shape((sec_pnl.shape[0] // TEAM, width), sec_pnl.dtype) for _ in range(TEAM - 1)), [VMEM]
     )(sec_pnl)
     others = [None] * (TEAM - 1)
-    for j in (3, 2, 1):
+    for j in range(TEAM - 1, 0, -1):
         others[j - 1] = lax.ppermute(packs[j - 1], "day", [(i, i ^ j) for i in range(n_day)])
     group = sec_pnl.shape[0] // TEAM
     wide, base, mine = call(
@@ -196,7 +206,7 @@
     pnl, sent = call(
         share_kernel, (shape((rows, width), jnp.bfloat16), shape((n_day, part + 8, PB), jnp.int16)), [VMEM] * 4
     )(arrived, mine, codes, meta)
-    back = exchange(sent, "day")
+    back = exchange(sent, "day", DAY_ROOT)
     tail_mean, short = call(tail_kernel, (shape((1, PB, SB), f32), shape((1, rows), f32)), [VMEM] * 2)(count, back)
     return pnl, short.reshape(rows), tail_mean
 

time: 48.5 us -> 43.3 us (0.89)
  waiting for transfers between devices: 2.82 us -> 0.01 us
  blocking collectives: 19 us -> 17.7 us
  starting transfers between devices: 19.4 us -> 18.5 us
    ppermute x3 -> x1, waiting for transfers between devices: 2.82 us -> 0.01 us  [step(): lax.ppermute(packs[j - 1], 'day', [(i, i ^ j) for i in range(n_day)])]
    ppermute x3 -> x1, starting transfers between devices: 8.78 us -> 6.27 us  [step(): lax.ppermute(packs[j - 1], 'day', [(i, i ^ j) for i in range(n_day)])]
    all_to_all x1, starting transfers between devices: 10.6 us -> 12.2 us  [exchange(): lax.all_to_all(x, axis, split_axis=0, concat_axis=0, tiled=True, axis_ind...]
    all_to_all x1, blocking collectives: 19 us -> 17.7 us  [exchange(): lax.all_to_all(x, axis, split_axis=0, concat_axis=0, tiled=True, axis_ind...]
  transfers between devices with their start and end apart: 4 -> 2, of which waited for: 1 -> 0; matrix products, arithmetic and copies ran while one was open for 0% -> 0% of each run, Pallas kernels for 4% -> 5%
where the time goes in v6:
time: 43.3 us; the launch traced here: 43.1 us
  starting transfers between devices  18.5 us (43%)
  blocking collectives  17.7 us (41%)
  Pallas kernels  5.47 us (13%)
  between operations  1.39 us (3%)
    all_to_all x1, blocking collectives, exchange(): lax.all_to_all(x, axis, split_axis=0, concat_axis=0, tiled=True, axis_ind...  17.7 us
    all_to_all x1, starting transfers between devices, exchange(): lax.all_to_all(x, axis, split_axis=0, concat_axis=0, tiled=True, axis_ind...  12.2 us
    ppermute x1, starting transfers between devices, step(): lax.ppermute(packs[j - 1], 'day', [(i, i ^ j) for i in range(n_day)])  6.27 us
    pallas_call x1, Pallas kernels, step(): call(partial_kernel, shape((portfolios, width), f32), [SMEM] * 2 + [VMEM]...  2.1 us
    pallas_call x1, Pallas kernels, step(): call(mask_kernel, (shape((TEAM * width, portfolios), jnp.bfloat16), shape...  1.02 us
    pallas_call x1, Pallas kernels, step(): call(codes_kernel, (shape((slots, part, PB), jnp.int16), shape((8, PB), f...  0.93 us
  transfers between devices with their start and end apart: 2, of which 0 were waited for; matrix products, arithmetic and copies ran while one was open for 0% of the time, Pallas kernels for 5%

profile of v6, /device:TPU:1, one launch (start us, length us, event | category | flops | bytes accessed | tf_op | source)
XLA Modules:
  0.0 43.1 jit_solution(2040250644887321241)
XLA Ops:
  1.3 2.1 %shard_map.85 = f32[256,128]{1,0:T(8,128)} custom-call(s32[16]{0:T(128)} %pb.5, s32[16]{0:T(128)} %sb.5, s32[1,1]{1,0:T(1,128)} %bitcast.4.cnt, bf16[1024,128]{1,0:T(8,128)(2,1)} %sec.3, bf16[16,128,128]{2,1,0:T(8,128)(2,1)} %hold.1), custom_call_target="tpu_custom_call" | custom-call | flops 10000000 | bytes 600000 | tf_op jit(solution)/shard_map/pallas_call | solution.py:179
  3.4 0.0 copy-start
  3.4 12.2 %all-to-all-start = ((f32[32,8,128]{2,1,0:T(8,128)}), f32[32,8,128]{2,1,0:T(8,128)S(1)}, u32[]{:S(2)}, u32[]{:S(2)}) async-start(f32[32,8,128]{2,1,0:T(8,128)} %bitcast.7), calls=%async_computation | async-start | bytes 262144 | tf_op jit(solution)/shard_map/all_to_all | solution.py:34
  15.6 0.0 copy-done
  15.6 0.0 copy-start.1
  15.6 0.0 copy-start.2
  15.7 0.0 copy-start.3
  15.7 6.3 %collective-permute-start = (bf16[512,128]{1,0:T(8,128)(2,1)S(1)}, bf16[512,128]{1,0:T(8,128)(2,1)S(1)}, u32[]{:S(2)}, u32[]{:S(2)}) collective-permute-start(bf16[512,128]{1,0:T(8,128)(2,1)S(1)} %shard_map.87), channel_id=1, source_target_pairs={{0,1},{1,0},{2,3},{3,2},{4,5},{5,4},{6,7},{7,6},{8,9},{9,8},{10,11... | collective-permute-start | bytes 393224 | tf_op jit(solution)/shard_map/ppermute | solution.py:192
  21.9 0.0 copy-done.1
  22.0 0.0 copy-done.2
  22.0 0.0 copy-done.3
  22.0 1.0 %shard_map.86 = (bf16[256,256]{1,0:T(8,128)(2,1)S(1)}, f32[512,256]{1,0:T(8,128)S(1)}, f32[8,128]{1,0:T(8,128)S(1)}) custom-call(s32[16]{0:T(128)S(1)} %copy-done.2, s32[16]{0:T(128)S(1)} %copy-done.3, s32[103,256]{1,0:T(8,128)S(1)} %bitcast.6, bf16[1024,128]{1,0:T(8,128)(2,1)S(1)} %copy-done), custom_call_target="tpu_custom_call" | custom-call | flops 10000000 | bytes 600000 | tf_op jit(solution)/shard_map/pallas_call | solution.py:194
  23.0 0.0 collective-permute-done.refs_0_
  23.0 0.9 %shard_map.88 = (s16[16,64,128]{2,1,0:T(8,128)(2,1)S(1)}, f32[8,128]{1,0:T(8,128)S(1)}) custom-call(s32[16]{0:T(128)S(1)} %copy-done.2, s32[16]{0:T(128)S(1)} %copy-done.3, bf16[256,256]{1,0:T(8,128)(2,1)S(1)} %get-tuple-element.13.wide, f32[512,256]{1,0:T(8,128)S(1)} %get-tuple-element.14.base, bf16[512,128]{1,0:T(8,128)(2,1)S(1)} %collective-permute-done.refs_0_), custom_call_target="tpu_custom_call" | custom-call | flops 10000000 | bytes 600000 | tf_op jit(solution)/shard_map/pallas_call | solution.py:200
  24.0 0.0 all-to-all-done.arrived
  24.0 0.6 %shard_map.89 = (bf16[8,128]{1,0:T(8,128)(2,1)}, s16[16,72,128]{2,1,0:T(8,128)(2,1)S(1)}) custom-call(f32[32,8,128]{2,1,0:T(8,128)S(1)} %all-to-all-done.arrived, f32[8,128]{1,0:T(8,128)S(1)} %get-tuple-element.12.mine, s16[16,64,128]{2,1,0:T(8,128)(2,1)S(1)} %get-tuple-element.15.codes, f32[8,128]{1,0:T(8,128)S(1)} %get-tuple-element.16.meta), custom_call_target="tpu_custom_call" | custom-call | flops 10000000 | bytes 600000 | tf_op jit(solution)/shard_map/pallas_call | solution.py:206
  24.6 17.7 %all_to_all.10.arrived = s16[16,72,128]{2,1,0:T(8,128)(2,1)S(1)} all-to-all(s16[16,72,128]{2,1,0:T(8,128)(2,1)S(1)} %get-tuple-element.18), channel_id=1, replica_groups={{12,13,14,15,0,1,2,3,4,5,6,7,8,9,10,11},{28,29,30,31,16,17,18,19,20,21,..., dimensions={0} | all-to-all | bytes 589824 | tf_op jit(solution)/shard_map/all_to_all | solution.py:34
  42.3 0.8 %shard_map.90 = (f32[1,128,128]{2,1,0:T(8,128)}, f32[1,8]{1,0:T(1,128)}) custom-call(s32[1,1]{1,0:T(1,128)} %bitcast.5.cnt, s16[16,72,128]{2,1,0:T(8,128)(2,1)S(1)} %all_to_all.10.arrived), custom_call_target="tpu_custom_call" | custom-call | flops 10000000 | bytes 600000 | tf_op jit(solution)/shard_map/pallas_call | solution.py:210
  (1 shorter events, 0.0 us)
Async XLA Ops:
  3.4 12.2 %copy-start = (bf16[1024,128]{1,0:T(8,128)(2,1)S(1)}, bf16[1024,128]{1,0:T(8,128)(2,1)}, u32[]{:S(2)}) copy-start(bf16[1024,128]{1,0:T(8,128)(2,1)} %sec.3) | copy-start | bytes 786436
  3.4 20.6 %all-to-all-start = ((f32[32,8,128]{2,1,0:T(8,128)}), f32[32,8,128]{2,1,0:T(8,128)S(1)}, u32[]{:S(2)}, u32[]{:S(2)}) async-start(f32[32,8,128]{2,1,0:T(8,128)} %bitcast.7), calls=%async_computation | async-start | bytes 262144 | tf_op jit(solution)/shard_map/all_to_all | solution.py:34
  15.6 6.4 %copy-start.1 = (s32[256,103]{0,1:T(8,128)S(1)}, s32[256,103]{0,1:T(8,128)}, u32[]{:S(2)}) copy-start(s32[256,103]{0,1:T(8,128)} %param.11) | copy-start | bytes 316420
  15.6 6.3 %copy-start.2 = (s32[16]{0:T(128)S(1)}, s32[16]{0:T(128)}, u32[]{:S(2)}) copy-start(s32[16]{0:T(128)} %pb.5) | copy-start | bytes 196
  15.7 6.3 %copy-start.3 = (s32[16]{0:T(128)S(1)}, s32[16]{0:T(128)}, u32[]{:S(2)}) copy-start(s32[16]{0:T(128)} %sb.5) | copy-start | bytes 196
  15.7 7.3 %collective-permute-start = (bf16[512,128]{1,0:T(8,128)(2,1)S(1)}, bf16[512,128]{1,0:T(8,128)(2,1)S(1)}, u32[]{:S(2)}, u32[]{:S(2)}) collective-permute-start(bf16[512,128]{1,0:T(8,128)(2,1)S(1)} %shard_map.87), channel_id=1, source_target_pairs={{0,1},{1,0},{2,3},{3,2},{4,5},{5,4},{6,7},{7,6},{8,9},{9,8},{10,11... | collective-permute-start | bytes 393224 | tf_op jit(solution)/shard_map/ppermute | solution.py:192
